TPU v7x, 32 devices: a whole 2x2x4 slice. The times are simulated.
32 devices in a mesh: blk: 8 (over z, core), section: 4 (over y, x).
Axes of the slice: x: 2, y: 2, z: 4, core: 2. Of those that a mesh axis runs over, the one named last changes fastest.
Arguments:
- hidden: bfloat16 [4, 2048, 4096], P('section', 'blk'), parts along dimension 1, may hold values from -6 to 6
- exit_layer: int32 [4096], P('blk'), parts along dimension 0, may hold values from 1 to 2
- lengths: int32 [4096], P('blk'), parts along dimension 0, may hold values from 1 to 16, as said below
- kv_cache: bfloat16 [4, 2048, 16, 256], P('section', 'blk'), parts along dimension 1, may hold values from -256 to 256
- norm_gain: bfloat16 [4, 4096], P('section'), may hold values from 0.5 to 1.5
- w_qkv: bfloat16 [4, 4096, 1280], P('section'), may hold values from -0.0625 to 0.0625
- w_out: bfloat16 [4, 1024, 4096], P('section'), may hold values from -0.1875 to 0.1875
Outputs:
- settled: bfloat16 [4096, 8192], P('blk', 'section'), parts along dimension 0
There are 8 independent parts, one for each index of `blk`. A program takes and returns all parts, laid end to end along the dimension named above; an argument that names none is the same for every part. Nothing has to cross between parts.
Inputs may be any that keep to these rules, and one draw needn't show every extreme that they name: `lengths`: some token has length 16.
All inputs are finite; a program needn't handle non-finite values.
Results may differ from a plain program's by a relative error of at most 0.03.
Values may be sent and summed in bfloat16 or wider, within the bound.
No kernel may reach another device: no remote copies, remote signals or barrier semaphores. Data moves between devices by JAX's collectives and lax.ppermute only.
A program may use at most 64 MiB of HBM per device.

v0:
```python
import functools
import math

import jax
import jax.numpy as jnp
from jax import lax
from jax.experimental import pallas as pl
from jax.experimental.pallas import tpu as pltpu
from jax.sharding import PartitionSpec as P


BLOCK = 64
MICRO = 8


EPSILON = 1e-05
NEGATIVE = -1e30


def partner(value, axis, distance):
    return lax.ppermute(value, axis, [(i, i ^ 1 << distance) for i in range(lax.axis_size(axis))])


def shifted(value, axis, steps):
    count = lax.axis_size(axis)
    pairs = [(source, (source + steps) % count) for source in range(count)]
    return lax.ppermute(value, axis, pairs)


def body(hidden, exit_layer, lengths, kv_cache, norm_gain, w_qkv, w_out):
    devices = lax.axis_size("section")
    index = lax.axis_index("section")
    shards = max(2, devices // 4)
    cycle_size = devices // shards
    segment_bits = cycle_size.bit_length() - 1
    shard_bits = shards.bit_length() - 1
    segment_index = index // shards
    shard_index = index % shards
    own_blocks = hidden[0]
    gain_row = norm_gain[0].astype(jnp.float32)
    proj_weight = w_qkv[0]
    out_weight = w_out[0]
    cache_all = kv_cache[0]
    query_width = out_weight.shape[0]
    head_size = (proj_weight.shape[1] - query_width) // 2
    heads = query_width // head_size
    quarter = proj_weight.shape[0]
    total_width = quarter * shards
    group_rows = BLOCK // shards
    rounds = MICRO // cycle_size
    context = cache_all.shape[1]
    positions = jnp.arange(context, dtype=jnp.int32)
    blank_block = jnp.zeros((BLOCK, quarter), jnp.bfloat16)

    def advance(carry, microstep):
        incoming, arriving, records = carry
        micro_index = microstep - segment_index
        in_range = (micro_index >= 0) & (micro_index < MICRO)
        slot = jnp.clip(micro_index, 0, MICRO - 1)
        on_turn = microstep % cycle_size == 0
        local_slot = jnp.minimum(microstep // cycle_size, rounds - 1)
        own_block = lax.dynamic_slice_in_dim(own_blocks, local_slot * BLOCK, BLOCK, 0)
        exit_rows = lax.dynamic_slice_in_dim(exit_layer, slot * BLOCK, BLOCK)
        own_lengths = lax.dynamic_slice_in_dim(
            lengths, slot * BLOCK + shard_index * group_rows, group_rows
        )
        own_cache = lax.dynamic_slice_in_dim(cache_all, slot * group_rows, group_rows, 0)
        first_input = jnp.where(on_turn, own_block, arriving)
        entering = jnp.where(segment_index == 0, first_input, incoming)
        active = exit_rows > segment_index
        gate = in_range & (jnp.sum(active.astype(jnp.int32)) > 0)

        def local_partials():
            widened = entering.astype(jnp.float32)
            scaled = (widened * gain_row).astype(jnp.bfloat16)
            return (
                jnp.dot(scaled, proj_weight, preferred_element_type=jnp.float32),
                jnp.sum(widened * widened, axis=1),
            )

        def no_partials():
            return (
                jnp.zeros((BLOCK, proj_weight.shape[1]), jnp.float32),
                jnp.zeros((BLOCK,), jnp.float32),
            )

        partial_proj, partial_squares = lax.cond(gate, local_partials, no_partials)
        kept = (partial_proj, partial_squares)
        for level in range(shard_bits):
            bit = shard_bits - 1 - level
            upper = index >> bit & 1
            halves = tuple(
                (piece.reshape((2, piece.shape[0] // 2) + piece.shape[1:]) for piece in kept)
            )
            keep = tuple((jnp.where(upper == 1, half[1], half[0]) for half in halves))
            send = tuple((jnp.where(upper == 1, half[0], half[1]) for half in halves))
            received = partner(send, "section", bit)
            kept = tuple((first + second for first, second in zip(keep, received)))
        own_proj, own_squares = kept

        def local_attention():
            fitted = own_proj * lax.rsqrt(own_squares / total_width + EPSILON)[:, None]
            query = (fitted[:, :query_width] * (1.0 / math.sqrt(head_size))).astype(jnp.bfloat16)
            query = query.reshape(group_rows, heads, head_size)
            key_new = fitted[:, query_width : query_width + head_size].astype(jnp.bfloat16)
            value_new = fitted[:, query_width + head_size :].astype(jnp.bfloat16)
            scores = jnp.einsum(
                "rhd,rcd->rhc",
                query,
                own_cache[:, :, :head_size],
                preferred_element_type=jnp.float32,
            )
            own = jnp.einsum("rhd,rd->rh", query, key_new, preferred_element_type=jnp.float32)
            usable = (positions[None, :] < own_lengths[:, None])[:, None, :]
            scores = jnp.where(usable, scores, NEGATIVE)
            row_top = jnp.maximum(jnp.max(scores, axis=-1), own)
            raw = jnp.where(usable, jnp.exp(scores - row_top[:, :, None]), jnp.float32(0.0))
            raw_own = jnp.exp(own - row_top)
            total = jnp.sum(raw, axis=-1) + raw_own
            weights = (raw / total[:, :, None]).astype(jnp.bfloat16)
            own_weight = (raw_own / total).astype(jnp.bfloat16)
            attended = jnp.einsum(
                "rhc,rcd->rhd",
                weights,
                own_cache[:, :, head_size:],
                preferred_element_type=jnp.float32,
            )
            attended = (
                attended
                + own_weight.astype(jnp.float32)[:, :, None]
                * value_new.astype(jnp.float32)[:, None, :]
            )
            return attended.astype(jnp.bfloat16).reshape(group_rows, query_width)

        def no_attention():
            return jnp.zeros((group_rows, query_width), jnp.bfloat16)

        collected = lax.cond(gate, local_attention, no_attention)
        for level in range(shard_bits):
            bit = level
            other = partner(collected, "section", bit)
            upper = index >> bit & 1
            collected = jnp.where(
                upper == 1,
                jnp.concatenate([other, collected], 0),
                jnp.concatenate([collected, other], 0),
            )

        def local_update():
            branch_out = jnp.dot(collected, out_weight, preferred_element_type=jnp.float32)
            updated = (entering.astype(jnp.float32) + branch_out).astype(jnp.bfloat16)
            return jnp.where(active[:, None], updated, entering)

        def keep_state():
            return entering

        outgoing = lax.cond(gate, local_update, keep_state)
        leaving = in_range & (exit_rows == segment_index + 1)
        previous = lax.dynamic_slice_in_dim(records, slot * BLOCK, BLOCK, 0)
        records = lax.dynamic_update_slice_in_dim(
            records, jnp.where(leaving[:, None], outgoing, previous), slot * BLOCK, 0
        )
        relayed = jnp.where(on_turn & (segment_index > 0), own_block, arriving)
        incoming, arriving = shifted((outgoing, relayed), "section", shards)
        return ((incoming, arriving, records), None)

    start = (blank_block, blank_block, jnp.zeros((MICRO * BLOCK, quarter), jnp.bfloat16))
    carry, _ = lax.scan(advance, start, jnp.arange(MICRO + cycle_size - 1, dtype=jnp.int32))
    kept = carry[2]
    for level in range(segment_bits):
        bit = shard_bits + segment_bits - 1 - level
        upper = index >> bit & 1
        halves = kept.reshape(kept.shape[0], 2, kept.shape[1] // 2)
        keep = jnp.where(upper == 1, halves[:, 1], halves[:, 0])
        send = jnp.where(upper == 1, halves[:, 0], halves[:, 1])
        received = partner(send, "section", bit)
        kept = (keep.astype(jnp.float32) + received.astype(jnp.float32)).astype(jnp.bfloat16)
    return kept


UNROLL = 1
AHEAD = 4
LIMIT = 6 * 1024 * 1024
CHUNKS = ((0, 2), (4, 6), (1, 3), (5, 7))
IN_VMEM = pl.BlockSpec(memory_space=pltpu.VMEM)
IN_SMEM = pl.BlockSpec(memory_space=pltpu.SMEM)
IN_HBM = pl.BlockSpec(memory_space=pltpu.HBM)


def call(kernel, inputs, in_specs, outs, out_specs=None, scratch=(), flops=10**8, **more):
    return pl.pallas_call(
        kernel,
        in_specs=in_specs,
        out_specs=[IN_VMEM] * len(outs) if out_specs is None else out_specs,
        out_shape=outs,
        scratch_shapes=scratch,
        compiler_params=pltpu.CompilerParams(vmem_limit_bytes=LIMIT),
        cost_estimate=pl.CostEstimate(flops=flops, bytes_accessed=10**6, transcendentals=0),
        **more,
    )(*inputs)


def seat():
    index = lax.axis_index("section")
    return index // 2, index % 2


def on_layer(layer, body_fn):
    upper, _ = seat()
    pl.when(upper == layer)(body_fn)


def exact_dot(a, b):
    return jnp.dot(
        a.astype(jnp.bfloat16), b.astype(jnp.bfloat16), preferred_element_type=jnp.float32
    )


def kept_rows(chunk):
    return len(CHUNKS[chunk]) * BLOCK // 2


def arrange_kernel(x_ref, order_ref, cache_ref, *refs):
    next_ref, held_cache_ref, outs, rows_ref, sem = refs[0], refs[1], refs[2:-2], refs[-2], refs[-1]
    tall = next_ref.shape[0]
    second = pltpu.make_async_copy(x_ref.at[pl.ds(tall, tall)], next_ref, sem.at[0])
    second.start()
    cache = pltpu.make_async_copy(cache_ref, held_cache_ref, sem.at[2])
    cache.start()
    tile = 512

    def select(chunk, source_ref, deep_ref, rest_ref):
        kept = deep_ref.shape[0]

        def each(i, carry):
            columns = pl.ds(pl.multiple_of(i * tile, tile), tile)
            rows = jnp.dot(
                order_ref[chunk], source_ref[:, columns], preferred_element_type=jnp.float32
            ).astype(jnp.bfloat16)
            deep_ref[:, columns] = rows[:kept]
            rest_ref[:, columns] = rows[kept:]
            return carry

        lax.fori_loop(0, x_ref.shape[1] // tile, each, 0)

    def upper():
        first = pltpu.make_async_copy(x_ref.at[pl.ds(0, tall)], rows_ref, sem.at[1])
        first.start()
        first.wait()
        select(2, rows_ref, outs[0], outs[2])

    on_layer(1, upper)
    second.wait()
    on_layer(1, functools.partial(select, 3, next_ref, outs[1], outs[3]))
    cache.wait()


def arrange(x, order, cache):
    tall, features = 2 * BLOCK, x.shape[1]
    return call(
        arrange_kernel, [x, order, cache], [IN_HBM, IN_VMEM, IN_HBM],
        [pltpu.VMEM((tall, features), x.dtype), pltpu.VMEM(cache.shape, cache.dtype)]
        + [pltpu.VMEM((BLOCK, features), x.dtype)] * 4,
        scratch=[pltpu.VMEM((tall, features), x.dtype), pltpu.SemaphoreType.DMA((3,))],
    )


def chunk_rows(values):
    lanes = lax.broadcasted_iota(jnp.int32, (1, 2 * BLOCK), 1)
    rows = []
    for blocks in CHUNKS:
        halves = []
        for side, block in enumerate(blocks):
            row = values[block // 2 : block // 2 + 1]
            halves.append(row if block % 2 == side else pltpu.roll(row, BLOCK, 1))
        if len(halves) == 1:
            halves.append(jnp.full_like(halves[0], -1.0))
        rows.append(jnp.where(lanes < BLOCK, halves[0], halves[1]))
    while len(rows) < 8:
        rows.append(jnp.full_like(rows[0], -1.0))
    return jnp.concatenate(rows, axis=0)


def prepare_kernel(exit_ref, length_ref, order_ref, restore_ref, active_ref, limit_ref, excess_ref):
    upper, shard = seat()
    tall = 2 * BLOCK
    half = BLOCK // 2
    values = chunk_rows(exit_ref[...].astype(jnp.float32))
    deep = (values > 1).astype(jnp.float32)
    rest = ((values >= 0) & (values <= 1)).astype(jnp.float32)
    first = lax.broadcasted_iota(jnp.int32, (tall, tall), 0)
    second = lax.broadcasted_iota(jnp.int32, (tall, tall), 1)
    ahead = (first <= second).astype(jnp.float32)
    counts = jnp.sum(deep, axis=1, keepdims=True)
    excess = jnp.int32(0)
    rank = jnp.where(deep > 0, exact_dot(deep, ahead) - 1, counts + exact_dot(rest, ahead) - 1)
    rank = jnp.where(values >= 0, rank, -1.0).astype(jnp.int32)
    for chunk in range(len(CHUNKS)):
        over = jnp.max(counts[chunk : chunk + 1]) > float(kept_rows(chunk))
        excess = jnp.maximum(excess, over.astype(jnp.int32))
        target = rank[chunk : chunk + 1]
        order = first == target
        order_ref[chunk] = order.astype(jnp.float32).astype(jnp.bfloat16)
        column = jnp.sum(
            jnp.where(first == second, target, 0).astype(jnp.float32), axis=1, keepdims=True
        )
        restore = column.astype(jnp.int32) == second
        restore_ref[chunk] = restore.astype(jnp.float32).astype(jnp.bfloat16)
        natural = (first == second) & (values[chunk : chunk + 1] > 0)
        ranked = order & (deep[chunk : chunk + 1] > 0)
        chosen = jnp.where(upper == 0, natural.astype(jnp.float32), ranked.astype(jnp.float32))
        active_ref[chunk] = jnp.broadcast_to(jnp.sum(chosen, axis=1, keepdims=True), (tall, 128))
    excess_ref[0] = excess
    context = limit_ref.shape[2] // half
    lengths = length_ref[...].astype(jnp.float32)
    lengths = jnp.concatenate([lengths, lengths], axis=0)
    source = lax.broadcasted_iota(jnp.int32, (tall, limit_ref.shape[2]), 0)
    column = lax.broadcasted_iota(jnp.int32, (tall, limit_ref.shape[2]), 1)
    for parity in range(2):
        spread = source == parity * BLOCK + shard * half + column // context
        limit_ref[parity] = exact_dot(lengths, spread.astype(jnp.float32))


def prepare(exits, lengths, context):
    tall = 2 * BLOCK
    count = len(CHUNKS)
    return call(
        prepare_kernel, [exits, lengths], [IN_VMEM] * 2,
        [
            pltpu.VMEM((count, tall, tall), jnp.bfloat16),
            pltpu.VMEM((count, tall, tall), jnp.bfloat16),
            pltpu.VMEM((count, tall, 128), jnp.float32),
            pltpu.VMEM((2, 8, BLOCK // 2 * context), jnp.float32),
            jax.ShapeDtypeStruct((1,), jnp.int32),
        ],
        [IN_VMEM] * 4 + [IN_SMEM],
    )


def own_rows(shard, piece):
    half = BLOCK // 2
    return pl.ds(pl.multiple_of(piece * BLOCK + shard * half, half), half)


def project_kernel(jobs, load, *refs):
    refs = list(refs)
    x_refs = [refs.pop(0) for _ in jobs]
    restore_ref = refs.pop(0) if any(kind != "all" for _, _, kind in jobs) else None
    gain_ref, w_ref = refs.pop(0), refs.pop(0)
    if load == "second":
        other_ref = refs.pop(0)
    keep_ref, keep_sq_ref, send_ref = refs.pop(0), refs.pop(0), refs.pop(0)
    if load:
        held_ref, sem = refs.pop(0), refs.pop()
    if load == "first":
        first_ref = refs.pop(0)
        first_rows = pltpu.make_async_copy(x_refs[0].at[pl.ds(0, first_ref.shape[0])], first_ref, sem.at[8])
        first_rows.start()
        x_refs = [first_ref]
    acc_ref, sq_ref = refs
    _, shard = seat()
    features = w_ref.shape[0]
    pieces = 8 if load == "first" else 2
    depth = features // pieces

    def fetch(i):
        rows = pl.ds(pl.multiple_of(i * depth, depth), depth)
        return pltpu.make_async_copy(w_ref.at[rows], held_ref.at[rows], sem.at[i])

    copies = []
    if load == "first":
        for i in range(AHEAD):
            fetch(i).start()
    elif load == "second":
        copies = [pltpu.make_async_copy(other_ref, held_ref, sem.at[0])]
    for copy in copies:
        copy.start()

    def multiply(layer, chunk, kind, x_ref):
        tall = len(CHUNKS[chunk]) * BLOCK

        def each(i, carry):
            columns = pl.ds(pl.multiple_of(i * depth, depth), depth)
            if kind != "all":
                base = tall // 2 if kind == "rest" else 0
                restore = restore_ref[chunk][:tall, base : base + tall // 2]
                x = jnp.dot(restore, x_ref[:, columns], preferred_element_type=jnp.float32)
            else:
                x = x_ref[:, columns].astype(jnp.float32)
            squares = None
            for lane in range(0, depth, 128):
                part = x[:, lane : lane + 128]
                squares = part * part if squares is None else squares + part * part
            scaled = (x * gain_ref[:, columns].astype(jnp.float32)).astype(jnp.bfloat16)
            if load == "first":
                fetch(i).wait()

                @pl.when(i + AHEAD < pieces)
                def _():
                    fetch(i + AHEAD).start()

                weight = held_ref[columns, :]
            else:
                weight = w_ref[columns, :]
            product = jnp.dot(scaled, weight, preferred_element_type=jnp.float32)
            acc_ref[:tall, :] += product
            sq_ref[:tall, :] += squares
            return carry

        acc_ref[:tall, :] = jnp.zeros((tall, acc_ref.shape[1]), jnp.float32)
        sq_ref[:tall, :] = jnp.zeros((tall, sq_ref.shape[1]), jnp.float32)
        lax.fori_loop(0, pieces, each, 0)
        half = BLOCK // 2
        width = keep_ref.shape[1]
        for piece in range(tall // BLOCK):
            here = own_rows(shard, piece)
            there = own_rows(1 - shard, piece)
            rows = pl.ds(piece * half, half)
            keep_ref[rows, :] = acc_ref[here, :]
            send_ref[rows, :width] = acc_ref[there, :].astype(jnp.bfloat16)
            own = jnp.sum(sq_ref[here, :], axis=1, keepdims=True)
            keep_sq_ref[rows, :] = jnp.broadcast_to(own, (half, 128))
            other = jnp.broadcast_to(jnp.sum(sq_ref[there, :], axis=1, keepdims=True), (half, 128))
            high = other.astype(jnp.bfloat16).astype(jnp.float32)
            lanes = lax.broadcasted_iota(jnp.int32, (half, 128), 1)
            send_ref[rows, width:] = jnp.where(lanes < 64, high, other - high).astype(jnp.bfloat16)

    if load == "first":
        first_rows.wait()
    for job, x_ref in zip(jobs, x_refs):
        if load == "first":
            multiply(*job, x_ref)
        else:
            on_layer(job[0], functools.partial(multiply, *job, x_ref))
    if load == "second":
        for copy in copies:
            copy.wait()


def widest(jobs):
    return max(len(CHUNKS[chunk]) for _, chunk, _ in jobs) * BLOCK


def project(jobs, xs, restore, gain, w, load=None, other=None):
    features, width = w.shape
    tall = widest(jobs)
    own = tall // 2
    pooled = any(kind != "all" for _, _, kind in jobs)
    inputs = list(xs) + [restore] * pooled + [gain, w]
    specs = [IN_VMEM] * len(inputs)
    outs = [
        pltpu.VMEM((own, width), jnp.float32),
        pltpu.VMEM((own, 128), jnp.float32),
        pltpu.VMEM((own, width + 128), jnp.bfloat16),
    ]
    scratch = [
        pltpu.VMEM((tall, width), jnp.float32),
        pltpu.VMEM((tall, 128), jnp.float32),
    ]
    if load == "first":
        specs[0] = specs[-1] = IN_HBM
        outs += [pltpu.VMEM(w.shape, w.dtype), pltpu.VMEM((tall, features), jnp.bfloat16)]
        scratch.append(pltpu.SemaphoreType.DMA((9,)))
    elif load == "second":
        inputs.append(other)
        specs.append(IN_HBM)
        outs.append(pltpu.VMEM(other.shape, other.dtype))
        scratch.append(pltpu.SemaphoreType.DMA((1,)))
    return call(
        functools.partial(project_kernel, jobs, load), inputs, specs, outs, scratch=scratch,
        flops=2 * tall * features * width,
    )


def attend_kernel(jobs, total_width, *refs):
    for layer, chunk, _ in jobs:
        on_layer(layer, functools.partial(attend_rows, chunk, total_width, *refs))


def attend_rows(chunk, total_width, keep_ref, keep_sq_ref, recv_ref, kv_ref, limit_ref, out_ref, fit_ref):
    width = keep_ref.shape[1]
    query_width = out_ref.shape[1]
    context = kv_ref.shape[1]
    head_size = kv_ref.shape[2] // 2
    heads = query_width // head_size
    half = BLOCK // 2
    tokens = 16
    columns = tokens * context
    count = len(CHUNKS[chunk]) * half
    other = recv_ref[:count, width:].astype(jnp.float32)
    squares = keep_sq_ref[:count, :1] + other[:, :1] + other[:, 64:65]
    factor = lax.rsqrt(squares / total_width + EPSILON)
    fitted = (keep_ref[:count, :] + recv_ref[:count, :width].astype(jnp.float32)) * factor
    scale = 1.0 / math.sqrt(head_size)
    fit_ref[:count, :query_width] = (fitted[:, :query_width] * scale).astype(jnp.bfloat16)
    fit_ref[:count, query_width:] = fitted[:, query_width:].astype(jnp.bfloat16)
    row = lax.broadcasted_iota(jnp.int32, (heads * tokens, columns), 0)
    column = lax.broadcasted_iota(jnp.int32, (heads * tokens, columns), 1)
    same = (row % tokens) == (column // context)
    position = (lax.broadcasted_iota(jnp.int32, (1, columns), 1) % context).astype(jnp.float32)
    pieces = [
        (place * half + part * tokens, block, part)
        for place, block in enumerate(CHUNKS[chunk])
        for part in range(half // tokens)
    ]
    queries, scores, owns, masks, tops, raws, raw_owns, totals = [], [], [], [], [], [], [], []
    for base, block, part in pieces:
        rows = slice(base, base + tokens)
        queries.append(
            jnp.concatenate(
                [fit_ref[rows, h * head_size : (h + 1) * head_size] for h in range(heads)], axis=0
            )
        )
    for i, (base, block, part) in enumerate(pieces):
        cached = slice(block * half + part * tokens, block * half + (part + 1) * tokens)
        keys = kv_ref[cached, :, :head_size].reshape(columns, head_size)
        scores.append(
            lax.dot_general(
                queries[i], keys, (((1,), (1,)), ((), ())), preferred_element_type=jnp.float32
            )
        )
        key_new = fit_ref[base : base + tokens, query_width : query_width + head_size]
        key_new = jnp.concatenate([key_new.astype(jnp.float32)] * heads, axis=0)
        owns.append(jnp.sum(queries[i].astype(jnp.float32) * key_new, axis=1, keepdims=True))
    for i, (base, block, part) in enumerate(pieces):
        line = block // 2
        limit = limit_ref[block % 2, line : line + 1, part * columns : (part + 1) * columns]
        masks.append(same & (position < limit))
        scores[i] = jnp.where(masks[i], scores[i], NEGATIVE)
        tops.append(jnp.maximum(jnp.max(scores[i], axis=1, keepdims=True), owns[i]))
    for i in range(len(pieces)):
        raws.append(jnp.where(masks[i], jnp.exp(scores[i] - tops[i]), 0.0))
        raw_owns.append(jnp.exp(owns[i] - tops[i]))
        totals.append(jnp.sum(raws[i], axis=1, keepdims=True) + raw_owns[i])
    for i, (base, block, part) in enumerate(pieces):
        rows = slice(base, base + tokens)
        cached = slice(block * half + part * tokens, block * half + (part + 1) * tokens)
        values = kv_ref[cached, :, head_size:].reshape(columns, head_size)
        weights = (raws[i] / totals[i]).astype(jnp.bfloat16)
        own_weight = (raw_owns[i] / totals[i]).astype(jnp.bfloat16).astype(jnp.float32)
        value_new = fit_ref[rows, query_width + head_size :].astype(jnp.float32)
        value_new = jnp.concatenate([value_new] * heads, axis=0)
        attended = jnp.dot(weights, values, preferred_element_type=jnp.float32)
        attended = (attended + own_weight * value_new).astype(jnp.bfloat16)
        for h in range(heads):
            out_ref[rows, h * head_size : (h + 1) * head_size] = attended[
                h * tokens : (h + 1) * tokens
            ]


def attend(jobs, total_width, keep, keep_sq, recv, kv, limits, query_width):
    own = keep.shape[0]
    return call(
        functools.partial(attend_kernel, jobs, total_width),
        [keep, keep_sq, recv, kv, limits], [IN_VMEM] * 5,
        [pltpu.VMEM((own, query_width), jnp.bfloat16)],
        scratch=[pltpu.VMEM((own, keep.shape[1]), jnp.bfloat16)],
        flops=900_000_000,
    )[0]


def output_kernel(jobs, own_ref, recv_ref, active_ref, order_ref, *refs):
    refs = list(refs)
    x_refs = [refs.pop(0) for _ in jobs]
    carry_ref = refs.pop(0) if jobs[-1][0] else None
    w_ref, att_ref = refs.pop(0), refs.pop()
    _, shard = seat()
    half = BLOCK // 2
    tile = 512
    middle = w_ref.shape[1] // 2

    def gather(tall):
        for piece in range(tall // BLOCK):
            rows = pl.ds(piece * half, half)
            att_ref[own_rows(shard, piece), :] = own_ref[rows, :]
            att_ref[own_rows(1 - shard, piece), :] = recv_ref[rows, :]

    def updated(chunk, x_ref, rows, columns, base=0):
        state = x_ref[:, columns].astype(jnp.float32)
        branch = jnp.dot(rows, w_ref[:, columns], preferred_element_type=jnp.float32)[: state.shape[0]]
        active = active_ref[chunk][base : base + state.shape[0], :1] > 0
        return jnp.where(active, state + branch, state).astype(jnp.bfloat16)

    def lower(chunk, x_ref, up_ref, high_rest_ref, low_rest_ref):
        tall = x_ref.shape[0]
        kept = tall // 2
        gather(tall)
        order = order_ref[chunk][:tall, :tall]

        def each(i, carry):
            inner = pl.ds(pl.multiple_of(i * tile, tile), tile)
            for side, rest_ref in enumerate((low_rest_ref, high_rest_ref)):
                columns = pl.ds(pl.multiple_of(i * tile + side * middle, tile), tile)
                state = updated(chunk, x_ref, att_ref[:tall, :], columns)
                ordered = jnp.dot(order, state, preferred_element_type=jnp.float32)
                up_ref[:, columns] = ordered[:kept].astype(jnp.bfloat16)
                rest_ref[:, inner] = ordered[kept:].astype(jnp.bfloat16)
            return carry

        lax.fori_loop(0, middle // tile, each, 0, unroll=UNROLL)

    def pooled(chunk, kind, x_ref, *outs):
        kept = x_ref.shape[0]
        tall = 2 * kept
        base = kept if kind == "rest" else 0
        gather(tall)
        rows = jnp.dot(
            order_ref[chunk][base : base + kept, :tall], att_ref[:tall, :], preferred_element_type=jnp.float32
        )
        att_ref[:kept, :] = rows.astype(jnp.bfloat16)

        def each(i, carry):
            inner = pl.ds(pl.multiple_of(i * tile, tile), tile)
            for side in range(2):
                columns = pl.ds(pl.multiple_of(i * tile + side * middle, tile), tile)
                state = updated(chunk, x_ref, att_ref[:tall, :], columns, base)
                if len(outs) == 1:
                    outs[0][:, columns] = state
                else:
                    outs[side][:, inner] = state
            return carry

        lax.fori_loop(0, middle // tile, each, 0, unroll=UNROLL)

    for (layer, chunk, kind), x_ref in zip(jobs, x_refs):
        outs = [refs.pop(0) for _ in range(len(result_shapes(layer, chunk, kind, 2 * middle)))]
        if kind == "all":
            on_layer(layer, functools.partial(lower, chunk, x_ref, *outs))
        else:
            on_layer(layer, functools.partial(pooled, chunk, kind, x_ref, *outs))
        if layer:
            swap_ref = outs[0]

            def ship():
                swap_ref[...] = carry_ref[...]

            on_layer(0, ship)


def result_shapes(layer, chunk, kind, features):
    kept = kept_rows(chunk)
    whole = pltpu.VMEM((kept, features), jnp.bfloat16)
    part = pltpu.VMEM((kept, features // 2), jnp.bfloat16)
    if layer or kind == "rest":
        return [part, part]
    return [whole, part, part] if kind == "all" else [whole]


def output(jobs, own, recv, active, order, xs, carry, w):
    depth, features = w.shape
    outs = []
    for job in jobs:
        outs += result_shapes(*job, features)
    inputs = [own, recv, active, order, *xs] + [carry] * jobs[-1][0] + [w]
    return call(
        functools.partial(output_kernel, jobs), inputs, [IN_VMEM] * len(inputs), outs,
        scratch=[pltpu.VMEM((widest(jobs), depth), jnp.bfloat16)],
        flops=2 * widest(jobs) * features * depth,
    )


def settle_rows(chunk, restore_ref, refs, rows_ref):
    received_ref, own_rest_ref, own_high_ref = refs
    tile = 512
    tall = rows_ref.shape[0]

    def place(first, rest):
        restore = restore_ref[chunk][:tall, :tall]

        def each(i, carry):
            columns = pl.ds(pl.multiple_of(i * tile, tile), tile)
            rows = jnp.concatenate([first[:, columns], rest[:, columns]], axis=0)
            rows_ref[:, columns] = jnp.dot(
                restore, rows, preferred_element_type=jnp.float32
            ).astype(jnp.bfloat16)
            return carry

        lax.fori_loop(0, rows_ref.shape[1] // tile, each, 0)

    on_layer(0, functools.partial(place, received_ref, own_rest_ref))
    on_layer(1, functools.partial(place, own_high_ref, received_ref))


def settle_kernel(jobs, restore_ref, *refs):
    outs = refs[3 * len(jobs) :]
    for i, chunk in enumerate(jobs):
        settle_rows(chunk, restore_ref, refs[3 * i : 3 * i + 3], outs[i])


def settled_shape(chunk, width):
    return pltpu.VMEM((len(CHUNKS[chunk]) * BLOCK, width), jnp.bfloat16)


def settle(jobs, restore, operands):
    width = operands[0].shape[1]
    inputs = [restore, *operands]
    return call(
        functools.partial(settle_kernel, jobs), inputs, [IN_VMEM] * len(inputs),
        [settled_shape(chunk, width) for chunk in jobs],
    )


def finish_kernel(jobs, restore_ref, *refs):
    count = len(CHUNKS) - len(jobs)
    ready, refs = refs[:count], refs[count:]
    operands, refs = refs[: 3 * len(jobs)], refs[3 * len(jobs) :]
    out_ref, rows_refs, sem = refs[0], refs[1:-1], refs[-1]
    started = []

    def put(chunk, rows_ref):
        for i, block in enumerate(CHUNKS[chunk]):
            copy = pltpu.make_async_copy(
                rows_ref.at[pl.ds(i * BLOCK, BLOCK)], out_ref.at[pl.ds(block * BLOCK, BLOCK)], sem.at[block]
            )
            copy.start()
            started.append(copy)

    for chunk in range(count):
        put(chunk, ready[chunk])
    for i, chunk in enumerate(jobs):
        settle_rows(chunk, restore_ref, operands[3 * i : 3 * i + 3], rows_refs[i])
        put(chunk, rows_refs[i])
    for copy in started:
        copy.wait()


def finish(jobs, restore, ready, operands, tokens):
    width = operands[0].shape[1]
    inputs = [restore, *ready, *operands]
    return call(
        functools.partial(finish_kernel, jobs), inputs, [IN_VMEM] * len(inputs),
        [pltpu.HBM((tokens, width), jnp.bfloat16)], [IN_HBM],
        scratch=[settled_shape(chunk, width) for chunk in jobs] + [pltpu.SemaphoreType.DMA((MICRO,))],
    )[0]


def hand_over_kernel(x_ref, out_ref):
    out_ref[...] = x_ref[...]


def hand_over(x):
    return call(hand_over_kernel, [x], [IN_VMEM], [jax.ShapeDtypeStruct(x.shape, x.dtype)])[0]


LAG = 3
SETTLES = ((0, 1), (2,), (3,))


def compact(hidden, exit_layer, lengths, kv_cache, norm_gain, w_qkv, w_out):
    swap = [(i, i ^ 1) for i in range(4)]
    up = [(0, 2), (1, 3)]
    down = [(2, 0), (3, 1)]
    across = [(i, i ^ 2) for i in range(4)]
    query_width = w_out.shape[1]
    total_width = float(2 * w_qkv.shape[1])
    count = len(CHUNKS)

    def send(value, pairs):
        return lax.ppermute(value, "section", pairs)

    order, restore, active, limits, excess = prepare(
        exit_layer.reshape(4, 2 * BLOCK), lengths.reshape(4, 2 * BLOCK), kv_cache.shape[2]
    )
    second, held_cache, *pooled = arrange(hidden[0], order, kv_cache[0])
    moved = [send(value, down) for value in pooled]
    entries = [hidden[0], second] + moved
    kinds = [(0, "all"), (1, "all"), (2, "deep"), (3, "deep"), (2, "rest"), (3, "rest")]
    arrived, settled, own_highs = [], [], []
    high_rests, low_rests = {}, {}
    queue = []

    def exchange(at, jobs, xs, keep, keep_sq, partial):
        received = send(partial, swap)
        own = attend(jobs, total_width, keep, keep_sq, received, held_cache, limits, query_width)
        other = send(own, swap)
        carry = high_rests[at - LAG] if at >= LAG else None
        results = list(output(jobs, own, other, active, order, xs, carry, held_out))
        for layer, chunk, kind in jobs:
            if layer:
                settled.append(send(results.pop(0), across))
                own_highs.append(results.pop(0))
                continue
            if kind != "rest":
                arrived.append(send(results.pop(0), up))
            if kind == "all":
                high_rests[chunk] = results.pop(0)
                low_rests[chunk] = results.pop(0)
            elif kind == "rest":
                low_rests[chunk] = results.pop(0)
                high_rests[chunk] = results.pop(0)

    for at in range(count + LAG):
        jobs, xs = [], []
        if at < len(kinds):
            jobs.append((0, *kinds[at]))
            xs.append(entries[at])
        if at >= LAG:
            jobs.append((1, at - LAG, "deep"))
            xs.append(arrived[at - LAG])
        if at == 0:
            *result, held_proj, first = project(jobs, xs, restore, norm_gain, w_qkv[0], "first")
            xs = [first]
        elif at == 1:
            *result, held_out = project(jobs, xs, restore, norm_gain, held_proj, "second", w_out[0])
        else:
            result = project(jobs, xs, restore, norm_gain, held_proj)
        queue.append((at, jobs, xs, *result))
        if at:
            for item in queue:
                exchange(*item)
            queue = []

    def settle_operands(chunks):
        return [
            value for c in chunks for value in (settled[c], low_rests[c], own_highs[c])
        ]

    ready = []
    for i, chunks in enumerate(SETTLES):
        if i + 1 < len(SETTLES):
            ready += settle(chunks, restore, settle_operands(chunks))
        else:
            out = finish(chunks, restore, ready, settle_operands(chunks), MICRO * BLOCK)
    arguments = (hidden, exit_layer, lengths, kv_cache, norm_gain, w_qkv, w_out)
    return lax.cond(excess[0] > 0, lambda out, *rest: hand_over(body(*rest)), lambda out, *rest: out, out, *arguments)


def solution(mesh):
    paired = mesh.shape["section"] == 4
    return jax.shard_map(
        compact if paired else body,
        mesh=mesh,
        in_specs=(
            P("section", "blk", None),
            P("blk"),
            P("blk"),
            P("section", "blk", None, None),
            P("section", None),
            P("section", None, None),
            P("section", None, None),
        ),
        out_specs=P("blk", "section"),
        check_vma=False,
    )
```

profile of v0, /device:TPU:0, one launch (start us, length us, event | category | flops | bytes accessed | tf_op | source)
XLA Modules:
  0.0 120.6 jit_solution(40769115115419722)
XLA Ops:
  0.0 7.2 %shard_map.77 = (f32[64,1280]{1,0:T(8,128)S(1)}, f32[64,128]{1,0:T(8,128)S(1)}, bf16[64,1408]{1,0:T(8,128)(2,1)S(1)}, bf16[4096,1280]{1,0:T(8,128)(2,1)S(1)}, bf16[128,4096]{1,0:T(8,128)(2,1)S(1)}) custom-call(bf16[256,4096]{1,0:T(8,128)(2,1)} %bitcast.42, bf16[1,4096]{1,0:T(2,128)(2,1)} %refs_2_.3, bf16[4096,1280]{1,0:T(8,128)(2,1)} %bitcast.36), custom_call_target="tpu_custom_call" | custom-call | flops 1342177280 | bytes 1000000 | tf_op jit(solution)/shard_map/pallas_call | solution.py:191
  7.2 3.0 %collective-permute-start.7 = (bf16[64,1408]{1,0:T(8,128)(2,1)S(1)}, bf16[64,1408]{1,0:T(8,128)(2,1)S(1)}, u32[]{:S(2)}, u32[]{:S(2)}) collective-permute-start(bf16[64,1408]{1,0:T(8,128)(2,1)S(1)} %get-tuple-element.525), channel_id=1, source_target_pairs={{0,1},{1,0},{2,3},{3,2},{4,5},{5,4},{6,7},{7,6},{8,9},{9,8},{10,11... | collective-permute-start | bytes 540680 | tf_op jit(solution)/shard_map/ppermute | solution.py:759
  10.2 1.4 %shard_map.75 = (bf16[4,128,128]{2,1,0:T(8,128)(2,1)S(1)}, bf16[4,128,128]{2,1,0:T(8,128)(2,1)S(1)}, f32[4,128,128]{2,1,0:T(8,128)S(1)}, f32[2,8,512]{2,1,0:T(8,128)S(1)}, s32[1]{0:T(128)}) custom-call(s32[4,128]{1,0:T(4,128)} %bitcast.55, s32[4,128]{1,0:T(4,128)S(1)} %bitcast.56), custom_call_target="tpu_custom_call" | custom-call | flops 100000000 | bytes 1000000 | tf_op jit(solution)/shard_map/pallas_call | solution.py:191
  11.9 2.8 %collective-permute-done.7.refs_2_ = bf16[64,1408]{1,0:T(8,128)(2,1)S(1)} collective-permute-done((bf16[64,1408]{1,0:T(8,128)(2,1)S(1)}, bf16[64,1408]{1,0:T(8,128)(2,1)S(1)}, u32[]{:S(2)}, u32[]{:S(2)}) %collective-permute-start.7) | collective-permute-done | bytes 180256 | tf_op jit(solution)/shard_map/ppermute | solution.py:759
  15.5 1.8 %collective-permute-start.8 = (bf16[64,1024]{1,0:T(8,128)(2,1)S(1)}, bf16[64,1024]{1,0:T(8,128)(2,1)S(1)}, u32[]{:S(2)}, u32[]{:S(2)}) collective-permute-start(bf16[64,1024]{1,0:T(8,128)(2,1)S(1)} %shard_map.78.own_ref), channel_id=1, source_target_pairs={{0,1},{1,0},{2,3},{3,2},{4,5},{5,4},{6,7},{7,6},{8,9},{9,8},{10,11... | collective-permute-start | bytes 393224 | tf_op jit(solution)/shard_map/ppermute | solution.py:759
  19.9 2.6 %shard_map.79 = (f32[64,1280]{1,0:T(8,128)S(1)}, f32[64,128]{1,0:T(8,128)S(1)}, bf16[64,1408]{1,0:T(8,128)(2,1)S(1)}, bf16[1024,4096]{1,0:T(8,128)(2,1)S(1)}) custom-call(bf16[128,4096]{1,0:T(8,128)(2,1)S(1)} %get-tuple-element.530.refs_0_, bf16[1,4096]{1,0:T(2,128)(2,1)S(1)} %copy-done.4, bf16[4096,1280]{1,0:T(8,128)(2,1)S(1)} %get-tuple-element.531.refs_2_.refs_4_.refs_3_, ...), custom_call_target="tpu_custom_call" | custom-call | flops 1342177280 | bytes 1000000 | tf_op jit(solution)/shard_map/pallas_call | solution.py:191
  22.5 3.2 %shard_map.80 = (bf16[64,4096]{1,0:T(8,128)(2,1)S(1)}, bf16[64,2048]{1,0:T(8,128)(2,1)S(1)}, bf16[64,2048]{1,0:T(8,128)(2,1)S(1)}) custom-call(bf16[64,1024]{1,0:T(8,128)(2,1)S(1)} %shard_map.78.own_ref, bf16[64,1024]{1,0:T(8,128)(2,1)S(1)} %collective-permute-done.8.recv_ref, f32[4,128,128]{2,1,0:T(8,128)S(1)} %get-tuple-element.528.active_ref, ...), custom_call_target="tpu_custom_call" | custom-call | flops 1073741824 | bytes 1000000 | tf_op jit(solution)/shard_map/pallas_call | solution.py:191
  25.7 1.3 %collective-permute-start.9 = (bf16[64,4096]{1,0:T(8,128)(2,1)S(1)}, bf16[64,4096]{1,0:T(8,128)(2,1)S(1)}, u32[]{:S(2)}, u32[]{:S(2)}) collective-permute-start(bf16[64,4096]{1,0:T(8,128)(2,1)S(1)} %get-tuple-element.533), channel_id=1, source_target_pairs={{0,2},{1,3},{4,6},{5,7},{8,10},{9,11},{12,14},{13,15},{16,18},{17,... | collective-permute-start | bytes 1572872 | tf_op jit(solution)/shard_map/ppermute | solution.py:759
  28.7 16.5 %collective-permute-done.21.refs_0_ = bf16[64,4096]{1,0:T(8,128)(2,1)S(1)} collective-permute-done((bf16[64,4096]{1,0:T(8,128)(2,1)S(1)}, bf16[64,4096]{1,0:T(8,128)(2,1)S(1)}, u32[]{:S(2)}, u32[]{:S(2)}) %collective-permute-start.21) | collective-permute-done | bytes 524320 | tf_op jit(solution)/shard_map/ppermute | solution.py:759
  45.2 2.4 %shard_map.90 = (f32[64,1280]{1,0:T(8,128)S(1)}, f32[64,128]{1,0:T(8,128)S(1)}, bf16[64,1408]{1,0:T(8,128)(2,1)S(1)}) custom-call(bf16[64,4096]{1,0:T(8,128)(2,1)S(1)} %collective-permute-done.21.refs_0_, bf16[4,128,128]{2,1,0:T(8,128)(2,1)S(1)} %get-tuple-element.520.refs_2_.restore_ref.refs_1_, bf16[1,4096]{1,0:T(2,128)(2,1)S(1)} %copy-done.4, ...), custom_call_target="tpu_custom_call" | custom-call | flops 1342177280 | bytes 1000000 | tf_op jit(solution)/shard_map/pallas_call | solution.py:191
  48.6 1.8 %collective-permute-start.15 = (bf16[64,1024]{1,0:T(8,128)(2,1)S(1)}, bf16[64,1024]{1,0:T(8,128)(2,1)S(1)}, u32[]{:S(2)}, u32[]{:S(2)}) collective-permute-start(bf16[64,1024]{1,0:T(8,128)(2,1)S(1)} %shard_map.84.own_ref), channel_id=1, source_target_pairs={{0,1},{1,0},{2,3},{3,2},{4,5},{5,4},{6,7},{7,6},{8,9},{9,8},{10,11... | collective-permute-start | bytes 393224 | tf_op jit(solution)/shard_map/ppermute | solution.py:759
  50.4 2.4 %shard_map.81 = (f32[64,1280]{1,0:T(8,128)S(1)}, f32[64,128]{1,0:T(8,128)S(1)}, bf16[64,1408]{1,0:T(8,128)(2,1)S(1)}) custom-call(bf16[64,4096]{1,0:T(8,128)(2,1)S(1)} %collective-permute-done.6.refs_0_, bf16[64,4096]{1,0:T(8,128)(2,1)S(1)} %collective-permute-done.9.refs_1_, bf16[4,128,128]{2,1,0:T(8,128)(2,1)S(1)} %get-tuple-element.520.refs_2_.restore_ref.refs_1_, ...), custom_call_target="tpu_custom_call" | custom-call | flops 1342177280 | bytes 1000000 | tf_op jit(solution)/shard_map/pallas_call | solution.py:191
  53.2 1.9 %collective-permute-done.22.refs_2_ = bf16[64,1408]{1,0:T(8,128)(2,1)S(1)} collective-permute-done((bf16[64,1408]{1,0:T(8,128)(2,1)S(1)}, bf16[64,1408]{1,0:T(8,128)(2,1)S(1)}, u32[]{:S(2)}, u32[]{:S(2)}) %collective-permute-start.22) | collective-permute-done | bytes 180256 | tf_op jit(solution)/shard_map/ppermute | solution.py:759
  57.2 3.2 %shard_map.85 = (bf16[64,4096]{1,0:T(8,128)(2,1)S(1)}, bf16[64,2048]{1,0:T(8,128)(2,1)S(1)}, bf16[64,2048]{1,0:T(8,128)(2,1)S(1)}) custom-call(bf16[64,1024]{1,0:T(8,128)(2,1)S(1)} %shard_map.84.own_ref, bf16[64,1024]{1,0:T(8,128)(2,1)S(1)} %collective-permute-done.15.recv_ref, f32[4,128,128]{2,1,0:T(8,128)S(1)} %get-tuple-element.528.active_ref, ...), custom_call_target="tpu_custom_call" | custom-call | flops 1073741824 | bytes 1000000 | tf_op jit(solution)/shard_map/pallas_call | solution.py:191
  60.4 1.3 %collective-permute-start.16 = (bf16[64,4096]{1,0:T(8,128)(2,1)S(1)}, bf16[64,4096]{1,0:T(8,128)(2,1)S(1)}, u32[]{:S(2)}, u32[]{:S(2)}) collective-permute-start(bf16[64,4096]{1,0:T(8,128)(2,1)S(1)} %get-tuple-element.545), channel_id=1, source_target_pairs={{0,2},{1,3},{4,6},{5,7},{8,10},{9,11},{12,14},{13,15},{16,18},{17,... | collective-permute-start | bytes 1572872 | tf_op jit(solution)/shard_map/ppermute | solution.py:759
  64.7 2.2 %shard_map.92 = bf16[64,4096]{1,0:T(8,128)(2,1)S(1)} custom-call(bf16[64,1024]{1,0:T(8,128)(2,1)S(1)} %shard_map.91.own_ref, bf16[64,1024]{1,0:T(8,128)(2,1)S(1)} %collective-permute-done.23.recv_ref, f32[4,128,128]{2,1,0:T(8,128)S(1)} %get-tuple-element.528.active_ref, bf16[4,128,128]{2,1,0:T(8,128)(2,1)S(1)} %get-tuple-element.521.order_ref, ...), custom_call_target="tpu_custom_call" | custom-call | flops 1073741824 | bytes 1000000 | tf_op jit(solution)/shard_map/pallas_call | solution.py:191
  66.9 2.5 %collective-permute-start.24 = (bf16[64,4096]{1,0:T(8,128)(2,1)S(1)}, bf16[64,4096]{1,0:T(8,128)(2,1)S(1)}, u32[]{:S(2)}, u32[]{:S(2)}) collective-permute-start(bf16[64,4096]{1,0:T(8,128)(2,1)S(1)} %shard_map.92), channel_id=1, source_target_pairs={{0,2},{1,3},{4,6},{5,7},{8,10},{9,11},{12,14},{13,15},{16,18},{17,... | collective-permute-start | bytes 1572872 | tf_op jit(solution)/shard_map/ppermute | solution.py:759
  69.3 2.2 %shard_map.83 = (bf16[64,4096]{1,0:T(8,128)(2,1)S(1)}, bf16[64,2048]{1,0:T(8,128)(2,1)S(1)}, bf16[64,2048]{1,0:T(8,128)(2,1)S(1)}) custom-call(bf16[64,1024]{1,0:T(8,128)(2,1)S(1)} %shard_map.82.own_ref, bf16[64,1024]{1,0:T(8,128)(2,1)S(1)} %collective-permute-done.11.recv_ref, f32[4,128,128]{2,1,0:T(8,128)S(1)} %get-tuple-element.528.active_ref, ...), custom_call_target="tpu_custom_call" | custom-call | flops 1073741824 | bytes 1000000 | tf_op jit(solution)/shard_map/pallas_call | solution.py:191
  71.5 1.5 %collective-permute-start.28 = (bf16[64,4096]{1,0:T(8,128)(2,1)S(1)}, bf16[64,4096]{1,0:T(8,128)(2,1)S(1)}, u32[]{:S(2)}, u32[]{:S(2)}) collective-permute-start(bf16[64,4096]{1,0:T(8,128)(2,1)S(1)} %get-tuple-element.567), channel_id=1, source_target_pairs={{0,2},{1,3},{4,6},{5,7},{8,10},{9,11},{12,14},{13,15},{16,18},{17,... | collective-permute-start | bytes 1572872 | tf_op jit(solution)/shard_map/ppermute | solution.py:759
  74.0 2.5 %shard_map.86 = (f32[64,1280]{1,0:T(8,128)S(1)}, f32[64,128]{1,0:T(8,128)S(1)}, bf16[64,1408]{1,0:T(8,128)(2,1)S(1)}) custom-call(bf16[64,4096]{1,0:T(8,128)(2,1)S(1)} %collective-permute-done.13.refs_0_, bf16[64,4096]{1,0:T(8,128)(2,1)S(1)} %collective-permute-done.16.refs_1_, bf16[4,128,128]{2,1,0:T(8,128)(2,1)S(1)} %get-tuple-element.520.refs_2_.restore_ref.refs_1_, ...), custom_call_target="tpu_custom_call" | custom-call | flops 1342177280 | bytes 1000000 | tf_op jit(solution)/shard_map/pallas_call | solution.py:191
  77.4 6.8 %collective-permute-done.24.refs_1_ = bf16[64,4096]{1,0:T(8,128)(2,1)S(1)} collective-permute-done((bf16[64,4096]{1,0:T(8,128)(2,1)S(1)}, bf16[64,4096]{1,0:T(8,128)(2,1)S(1)}, u32[]{:S(2)}, u32[]{:S(2)}) %collective-permute-start.24) | collective-permute-done | bytes 524320 | tf_op jit(solution)/shard_map/ppermute | solution.py:759
  84.3 2.5 %shard_map.93 = (f32[64,1280]{1,0:T(8,128)S(1)}, f32[64,128]{1,0:T(8,128)S(1)}, bf16[64,1408]{1,0:T(8,128)(2,1)S(1)}) custom-call(bf16[64,4096]{1,0:T(8,128)(2,1)S(1)} %collective-permute-done.20.refs_0_, bf16[64,4096]{1,0:T(8,128)(2,1)S(1)} %collective-permute-done.24.refs_1_, bf16[4,128,128]{2,1,0:T(8,128)(2,1)S(1)} %get-tuple-element.520.refs_2_.restore_ref.refs_1_, ...), custom_call_target="tpu_custom_call" | custom-call | flops 1342177280 | bytes 1000000 | tf_op jit(solution)/shard_map/pallas_call | solution.py:191
  88.0 1.9 %collective-permute-done.28.refs_0_ = bf16[64,4096]{1,0:T(8,128)(2,1)S(1)} collective-permute-done((bf16[64,4096]{1,0:T(8,128)(2,1)S(1)}, bf16[64,4096]{1,0:T(8,128)(2,1)S(1)}, u32[]{:S(2)}, u32[]{:S(2)}) %collective-permute-start.28) | collective-permute-done | bytes 524320 | tf_op jit(solution)/shard_map/ppermute | solution.py:759
  92.7 5.0 %collective-permute-start.12 = (bf16[64,2048]{1,0:T(8,128)(2,1)S(1)}, bf16[64,2048]{1,0:T(8,128)(2,1)S(1)}, u32[]{:S(2)}, u32[]{:S(2)}) collective-permute-start(bf16[64,2048]{1,0:T(8,128)(2,1)S(1)} %get-tuple-element.538), channel_id=1, source_target_pairs={{0,2},{1,3},{2,0},{3,1},{4,6},{5,7},{6,4},{7,5},{8,10},{9,11},{10,... | collective-permute-start | bytes 786440 | tf_op jit(solution)/shard_map/ppermute | solution.py:759
  100.4 2.2 %shard_map.88 = (bf16[64,2048]{1,0:T(8,128)(2,1)S(1)}, bf16[64,2048]{1,0:T(8,128)(2,1)S(1)}, bf16[64,2048]{1,0:T(8,128)(2,1)S(1)}, bf16[64,2048]{1,0:T(8,128)(2,1)S(1)}) custom-call(bf16[64,1024]{1,0:T(8,128)(2,1)S(1)} %shard_map.87.own_ref, bf16[64,1024]{1,0:T(8,128)(2,1)S(1)} %collective-permute-done.18.recv_ref, ...), custom_call_target="tpu_custom_call" | custom-call | flops 1073741824 | bytes 1000000 | tf_op jit(solution)/shard_map/pallas_call | solution.py:191
  102.6 2.8 %collective-permute-start.19 = (bf16[64,2048]{1,0:T(8,128)(2,1)S(1)}, bf16[64,2048]{1,0:T(8,128)(2,1)S(1)}, u32[]{:S(2)}, u32[]{:S(2)}) collective-permute-start(bf16[64,2048]{1,0:T(8,128)(2,1)S(1)} %get-tuple-element.550), channel_id=1, source_target_pairs={{0,2},{1,3},{2,0},{3,1},{4,6},{5,7},{6,4},{7,5},{8,10},{9,11},{10,... | collective-permute-start | bytes 786440 | tf_op jit(solution)/shard_map/ppermute | solution.py:759
  105.4 2.1 %shard_map.95 = (bf16[64,2048]{1,0:T(8,128)(2,1)S(1)}, bf16[64,2048]{1,0:T(8,128)(2,1)S(1)}, bf16[64,2048]{1,0:T(8,128)(2,1)S(1)}, bf16[64,2048]{1,0:T(8,128)(2,1)S(1)}) custom-call(bf16[64,1024]{1,0:T(8,128)(2,1)S(1)} %shard_map.94.own_ref, bf16[64,1024]{1,0:T(8,128)(2,1)S(1)} %collective-permute-done.26.recv_ref, ...), custom_call_target="tpu_custom_call" | custom-call | flops 1073741824 | bytes 1000000 | tf_op jit(solution)/shard_map/pallas_call | solution.py:191
  107.7 4.2 %collective-permute-start.31 = (bf16[64,2048]{1,0:T(8,128)(2,1)S(1)}, bf16[64,2048]{1,0:T(8,128)(2,1)S(1)}, u32[]{:S(2)}, u32[]{:S(2)}) collective-permute-start(bf16[64,2048]{1,0:T(8,128)(2,1)S(1)} %get-tuple-element.572), channel_id=1, source_target_pairs={{0,2},{1,3},{2,0},{3,1},{4,6},{5,7},{6,4},{7,5},{8,10},{9,11},{10,... | collective-permute-start | bytes 786440 | tf_op jit(solution)/shard_map/ppermute | solution.py:759
  112.6 1.4 %shard_map.89 = (bf16[128,2048]{1,0:T(8,128)(2,1)S(1)}, bf16[128,2048]{1,0:T(8,128)(2,1)S(1)}) custom-call(bf16[4,128,128]{2,1,0:T(8,128)(2,1)S(1)} %get-tuple-element.520.refs_2_.restore_ref.refs_1_, bf16[64,2048]{1,0:T(8,128)(2,1)S(1)} %collective-permute-done.12.refs_0_, bf16[64,2048]{1,0:T(8,128)(2,1)S(1)} %get-tuple-element.539.refs_1_, ...), custom_call_target="tpu_custom_call" | custom-call | flops 100000000 | bytes 1000000 | tf_op jit(solution)/shard_map/pallas_call | solution.py:191
  114.0 1.9 %collective-permute-done.27.refs_0_ = bf16[64,2048]{1,0:T(8,128)(2,1)S(1)} collective-permute-done((bf16[64,2048]{1,0:T(8,128)(2,1)S(1)}, bf16[64,2048]{1,0:T(8,128)(2,1)S(1)}, u32[]{:S(2)}, u32[]{:S(2)}) %collective-permute-start.27) | collective-permute-done | bytes 262176 | tf_op jit(solution)/shard_map/ppermute | solution.py:759
  116.6 2.1 %collective-permute-done.31.refs_3_ = bf16[64,2048]{1,0:T(8,128)(2,1)S(1)} collective-permute-done((bf16[64,2048]{1,0:T(8,128)(2,1)S(1)}, bf16[64,2048]{1,0:T(8,128)(2,1)S(1)}, u32[]{:S(2)}, u32[]{:S(2)}) %collective-permute-start.31) | collective-permute-done | bytes 262176 | tf_op jit(solution)/shard_map/ppermute | solution.py:759
  118.6 1.6 %shard_map.100 = bf16[512,2048]{1,0:T(8,128)(2,1)} custom-call(bf16[4,128,128]{2,1,0:T(8,128)(2,1)S(1)} %get-tuple-element.520.refs_2_.restore_ref.refs_1_, bf16[128,2048]{1,0:T(8,128)(2,1)S(1)} %get-tuple-element.553.refs_0_, bf16[128,2048]{1,0:T(8,128)(2,1)S(1)} %get-tuple-element.554.refs_1_, bf16[128,2048]{1,0:T(8,128)(2,1)S(1)} %shard_map.96.refs_2_, ...), custom_call_target="tpu_custom_call" | custom-call | flops 100000000 | bytes 1000000 | tf_op jit(solution)/shard_map/pallas_call | solution.py:191
  (60 shorter events, 21.3 us)
Async XLA Ops:
  0.0 19.9 %slice-start = ((s8[8388608]{0:T(1024)(128)(4,1)}), s8[4194304]{0:T(1024)(128)(4,1)S(1)}, s32[]{:S(2)}) async-start(s8[8388608]{0:T(1024)(128)(4,1)} %bitcast.38), calls=%async_computation | async-start | bytes 8388608
  0.0 10.2 %copy-start.8 = (s32[512]{0:T(512)S(1)}, s32[512]{0:T(512)}, u32[]{:S(2)}) copy-start(s32[512]{0:T(512)} %param.19) | copy-start | bytes 6148
  0.0 11.6 %copy-start = (bf16[1,256,4096]{2,1,0:T(8,128)(2,1)S(1)}, bf16[1,256,4096]{2,1,0:T(8,128)(2,1)}, u32[]{:S(2)}) copy-start(bf16[1,256,4096]{2,1,0:T(8,128)(2,1)} %param.17) | copy-start | bytes 6291460
  0.0 11.6 %copy-start.3 = (bf16[1,256,16,256]{3,2,1,0:T(8,128)(2,1)S(1)}, bf16[1,256,16,256]{3,2,1,0:T(8,128)(2,1)}, u32[]{:S(2)}) copy-start(bf16[1,256,16,256]{3,2,1,0:T(8,128)(2,1)} %param.20) | copy-start | bytes 6291460
  0.0 19.9 %slice-start.1 = ((s8[8388608]{0:T(1024)(128)(4,1)}), s8[4194304]{0:T(1024)(128)(4,1)S(1)}, s32[]{:S(2)}) async-start(s8[8388608]{0:T(1024)(128)(4,1)} %bitcast.38), calls=%async_computation.1 | async-start | bytes 8388608
  7.2 7.6 %collective-permute-start.7 = (bf16[64,1408]{1,0:T(8,128)(2,1)S(1)}, bf16[64,1408]{1,0:T(8,128)(2,1)S(1)}, u32[]{:S(2)}, u32[]{:S(2)}) collective-permute-start(bf16[64,1408]{1,0:T(8,128)(2,1)S(1)} %get-tuple-element.525), channel_id=1, source_target_pairs={{0,1},{1,0},{2,3},{3,2},{4,5},{5,4},{6,7},{7,6},{8,9},{9,8},{10,11... | collective-permute-start | bytes 540680 | tf_op jit(solution)/shard_map/ppermute | solution.py:759
  11.9 8.0 %copy-start.4 = (bf16[1,4096]{1,0:T(2,128)(2,1)S(1)}, bf16[1,4096]{1,0:T(2,128)(2,1)}, u32[]{:S(2)}) copy-start(bf16[1,4096]{1,0:T(2,128)(2,1)} %refs_2_.3) | copy-start | bytes 24580
  15.5 7.0 %collective-permute-start.8 = (bf16[64,1024]{1,0:T(8,128)(2,1)S(1)}, bf16[64,1024]{1,0:T(8,128)(2,1)S(1)}, u32[]{:S(2)}, u32[]{:S(2)}) collective-permute-start(bf16[64,1024]{1,0:T(8,128)(2,1)S(1)} %shard_map.78.own_ref), channel_id=1, source_target_pairs={{0,1},{1,0},{2,3},{3,2},{4,5},{5,4},{6,7},{7,6},{8,9},{9,8},{10,11... | collective-permute-start | bytes 393224 | tf_op jit(solution)/shard_map/ppermute | solution.py:759
  17.3 33.2 %collective-permute-start.6 = (bf16[64,4096]{1,0:T(8,128)(2,1)S(1)}, bf16[64,4096]{1,0:T(8,128)(2,1)S(1)}, u32[]{:S(2)}, u32[]{:S(2)}) collective-permute-start(bf16[64,4096]{1,0:T(8,128)(2,1)S(1)} %get-tuple-element.522), channel_id=1, source_target_pairs={{2,0},{3,1},{6,4},{7,5},{10,8},{11,9},{14,12},{15,13},{18,16},{19,... | collective-permute-start | bytes 1572872 | tf_op jit(solution)/shard_map/ppermute | solution.py:759
  18.6 26.6 %collective-permute-start.21 = (bf16[64,4096]{1,0:T(8,128)(2,1)S(1)}, bf16[64,4096]{1,0:T(8,128)(2,1)S(1)}, u32[]{:S(2)}, u32[]{:S(2)}) collective-permute-start(bf16[64,4096]{1,0:T(8,128)(2,1)S(1)} %get-tuple-element.556), channel_id=1, source_target_pairs={{2,0},{3,1},{6,4},{7,5},{10,8},{11,9},{14,12},{15,13},{18,16},{19,... | collective-permute-start | bytes 1572872 | tf_op jit(solution)/shard_map/ppermute | solution.py:759
  25.7 24.7 %collective-permute-start.9 = (bf16[64,4096]{1,0:T(8,128)(2,1)S(1)}, bf16[64,4096]{1,0:T(8,128)(2,1)S(1)}, u32[]{:S(2)}, u32[]{:S(2)}) collective-permute-start(bf16[64,4096]{1,0:T(8,128)(2,1)S(1)} %get-tuple-element.533), channel_id=1, source_target_pairs={{0,2},{1,3},{4,6},{5,7},{8,10},{9,11},{12,14},{13,15},{16,18},{17,... | collective-permute-start | bytes 1572872 | tf_op jit(solution)/shard_map/ppermute | solution.py:759
  27.0 20.9 %collective-permute-start.14 = (bf16[64,1408]{1,0:T(8,128)(2,1)S(1)}, bf16[64,1408]{1,0:T(8,128)(2,1)S(1)}, u32[]{:S(2)}, u32[]{:S(2)}) collective-permute-start(bf16[64,1408]{1,0:T(8,128)(2,1)S(1)} %get-tuple-element.544), channel_id=1, source_target_pairs={{0,1},{1,0},{2,3},{3,2},{4,5},{5,4},{6,7},{7,6},{8,9},{9,8},{10,11... | collective-permute-start | bytes 540680 | tf_op jit(solution)/shard_map/ppermute | solution.py:759
  27.4 45.6 %collective-permute-start.13 = (bf16[64,4096]{1,0:T(8,128)(2,1)S(1)}, bf16[64,4096]{1,0:T(8,128)(2,1)S(1)}, u32[]{:S(2)}, u32[]{:S(2)}) collective-permute-start(bf16[64,4096]{1,0:T(8,128)(2,1)S(1)} %get-tuple-element.541), channel_id=1, source_target_pairs={{2,0},{3,1},{6,4},{7,5},{10,8},{11,9},{14,12},{15,13},{18,16},{19,... | collective-permute-start | bytes 1572872 | tf_op jit(solution)/shard_map/ppermute | solution.py:759
  47.6 7.5 %collective-permute-start.22 = (bf16[64,1408]{1,0:T(8,128)(2,1)S(1)}, bf16[64,1408]{1,0:T(8,128)(2,1)S(1)}, u32[]{:S(2)}, u32[]{:S(2)}) collective-permute-start(bf16[64,1408]{1,0:T(8,128)(2,1)S(1)} %get-tuple-element.559), channel_id=1, source_target_pairs={{0,1},{1,0},{2,3},{3,2},{4,5},{5,4},{6,7},{7,6},{8,9},{9,8},{10,11... | collective-permute-start | bytes 540680 | tf_op jit(solution)/shard_map/ppermute | solution.py:759
  48.6 8.6 %collective-permute-start.15 = (bf16[64,1024]{1,0:T(8,128)(2,1)S(1)}, bf16[64,1024]{1,0:T(8,128)(2,1)S(1)}, u32[]{:S(2)}, u32[]{:S(2)}) collective-permute-start(bf16[64,1024]{1,0:T(8,128)(2,1)S(1)} %shard_map.84.own_ref), channel_id=1, source_target_pairs={{0,1},{1,0},{2,3},{3,2},{4,5},{5,4},{6,7},{7,6},{8,9},{9,8},{10,11... | collective-permute-start | bytes 393224 | tf_op jit(solution)/shard_map/ppermute | solution.py:759
  52.9 8.9 %collective-permute-start.10 = (bf16[64,1408]{1,0:T(8,128)(2,1)S(1)}, bf16[64,1408]{1,0:T(8,128)(2,1)S(1)}, u32[]{:S(2)}, u32[]{:S(2)}) collective-permute-start(bf16[64,1408]{1,0:T(8,128)(2,1)S(1)} %get-tuple-element.536), channel_id=1, source_target_pairs={{0,1},{1,0},{2,3},{3,2},{4,5},{5,4},{6,7},{7,6},{8,9},{9,8},{10,11... | collective-permute-start | bytes 540680 | tf_op jit(solution)/shard_map/ppermute | solution.py:759
  55.8 8.9 %collective-permute-start.23 = (bf16[64,1024]{1,0:T(8,128)(2,1)S(1)}, bf16[64,1024]{1,0:T(8,128)(2,1)S(1)}, u32[]{:S(2)}, u32[]{:S(2)}) collective-permute-start(bf16[64,1024]{1,0:T(8,128)(2,1)S(1)} %shard_map.91.own_ref), channel_id=1, source_target_pairs={{0,1},{1,0},{2,3},{3,2},{4,5},{5,4},{6,7},{7,6},{8,9},{9,8},{10,11... | collective-permute-start | bytes 393224 | tf_op jit(solution)/shard_map/ppermute | solution.py:759
  60.4 13.6 %collective-permute-start.16 = (bf16[64,4096]{1,0:T(8,128)(2,1)S(1)}, bf16[64,4096]{1,0:T(8,128)(2,1)S(1)}, u32[]{:S(2)}, u32[]{:S(2)}) collective-permute-start(bf16[64,4096]{1,0:T(8,128)(2,1)S(1)} %get-tuple-element.545), channel_id=1, source_target_pairs={{0,2},{1,3},{4,6},{5,7},{8,10},{9,11},{12,14},{13,15},{16,18},{17,... | collective-permute-start | bytes 1572872 | tf_op jit(solution)/shard_map/ppermute | solution.py:759
  62.5 6.9 %collective-permute-start.11 = (bf16[64,1024]{1,0:T(8,128)(2,1)S(1)}, bf16[64,1024]{1,0:T(8,128)(2,1)S(1)}, u32[]{:S(2)}, u32[]{:S(2)}) collective-permute-start(bf16[64,1024]{1,0:T(8,128)(2,1)S(1)} %shard_map.82.own_ref), channel_id=1, source_target_pairs={{0,1},{1,0},{2,3},{3,2},{4,5},{5,4},{6,7},{7,6},{8,9},{9,8},{10,11... | collective-permute-start | bytes 393224 | tf_op jit(solution)/shard_map/ppermute | solution.py:759
  63.4 14.1 %collective-permute-start.20 = (bf16[64,4096]{1,0:T(8,128)(2,1)S(1)}, bf16[64,4096]{1,0:T(8,128)(2,1)S(1)}, u32[]{:S(2)}, u32[]{:S(2)}) collective-permute-start(bf16[64,4096]{1,0:T(8,128)(2,1)S(1)} %get-tuple-element.555), channel_id=1, source_target_pairs={{2,0},{3,1},{6,4},{7,5},{10,8},{11,9},{14,12},{15,13},{18,16},{19,... | collective-permute-start | bytes 1572872 | tf_op jit(solution)/shard_map/ppermute | solution.py:759
  66.9 17.4 %collective-permute-start.24 = (bf16[64,4096]{1,0:T(8,128)(2,1)S(1)}, bf16[64,4096]{1,0:T(8,128)(2,1)S(1)}, u32[]{:S(2)}, u32[]{:S(2)}) collective-permute-start(bf16[64,4096]{1,0:T(8,128)(2,1)S(1)} %shard_map.92), channel_id=1, source_target_pairs={{0,2},{1,3},{4,6},{5,7},{8,10},{9,11},{12,14},{13,15},{16,18},{17,... | collective-permute-start | bytes 1572872 | tf_op jit(solution)/shard_map/ppermute | solution.py:759
  71.5 18.4 %collective-permute-start.28 = (bf16[64,4096]{1,0:T(8,128)(2,1)S(1)}, bf16[64,4096]{1,0:T(8,128)(2,1)S(1)}, u32[]{:S(2)}, u32[]{:S(2)}) collective-permute-start(bf16[64,4096]{1,0:T(8,128)(2,1)S(1)} %get-tuple-element.567), channel_id=1, source_target_pairs={{0,2},{1,3},{4,6},{5,7},{8,10},{9,11},{12,14},{13,15},{16,18},{17,... | collective-permute-start | bytes 1572872 | tf_op jit(solution)/shard_map/ppermute | solution.py:759
  76.5 14.5 %collective-permute-start.17 = (bf16[64,1408]{1,0:T(8,128)(2,1)S(1)}, bf16[64,1408]{1,0:T(8,128)(2,1)S(1)}, u32[]{:S(2)}, u32[]{:S(2)}) collective-permute-start(bf16[64,1408]{1,0:T(8,128)(2,1)S(1)} %get-tuple-element.548), channel_id=1, source_target_pairs={{0,1},{1,0},{2,3},{3,2},{4,5},{5,4},{6,7},{7,6},{8,9},{9,8},{10,11... | collective-permute-start | bytes 540680 | tf_op jit(solution)/shard_map/ppermute | solution.py:759
  86.8 10.8 %collective-permute-start.25 = (bf16[64,1408]{1,0:T(8,128)(2,1)S(1)}, bf16[64,1408]{1,0:T(8,128)(2,1)S(1)}, u32[]{:S(2)}, u32[]{:S(2)}) collective-permute-start(bf16[64,1408]{1,0:T(8,128)(2,1)S(1)} %get-tuple-element.562), channel_id=1, source_target_pairs={{0,1},{1,0},{2,3},{3,2},{4,5},{5,4},{6,7},{7,6},{8,9},{9,8},{10,11... | collective-permute-start | bytes 540680 | tf_op jit(solution)/shard_map/ppermute | solution.py:759
  89.9 9.7 %collective-permute-start.29 = (bf16[64,1408]{1,0:T(8,128)(2,1)S(1)}, bf16[64,1408]{1,0:T(8,128)(2,1)S(1)}, u32[]{:S(2)}, u32[]{:S(2)}) collective-permute-start(bf16[64,1408]{1,0:T(8,128)(2,1)S(1)} %get-tuple-element.570), channel_id=1, source_target_pairs={{0,1},{1,0},{2,3},{3,2},{4,5},{5,4},{6,7},{7,6},{8,9},{9,8},{10,11... | collective-permute-start | bytes 540680 | tf_op jit(solution)/shard_map/ppermute | solution.py:759
  91.7 8.7 %collective-permute-start.18 = (bf16[64,1024]{1,0:T(8,128)(2,1)S(1)}, bf16[64,1024]{1,0:T(8,128)(2,1)S(1)}, u32[]{:S(2)}, u32[]{:S(2)}) collective-permute-start(bf16[64,1024]{1,0:T(8,128)(2,1)S(1)} %shard_map.87.own_ref), channel_id=1, source_target_pairs={{0,1},{1,0},{2,3},{3,2},{4,5},{5,4},{6,7},{7,6},{8,9},{9,8},{10,11... | collective-permute-start | bytes 393224 | tf_op jit(solution)/shard_map/ppermute | solution.py:759
  92.7 19.8 %collective-permute-start.12 = (bf16[64,2048]{1,0:T(8,128)(2,1)S(1)}, bf16[64,2048]{1,0:T(8,128)(2,1)S(1)}, u32[]{:S(2)}, u32[]{:S(2)}) collective-permute-start(bf16[64,2048]{1,0:T(8,128)(2,1)S(1)} %get-tuple-element.538), channel_id=1, source_target_pairs={{0,2},{1,3},{2,0},{3,1},{4,6},{5,7},{6,4},{7,5},{8,10},{9,11},{10,... | collective-permute-start | bytes 786440 | tf_op jit(solution)/shard_map/ppermute | solution.py:759
  98.3 7.1 %collective-permute-start.26 = (bf16[64,1024]{1,0:T(8,128)(2,1)S(1)}, bf16[64,1024]{1,0:T(8,128)(2,1)S(1)}, u32[]{:S(2)}, u32[]{:S(2)}) collective-permute-start(bf16[64,1024]{1,0:T(8,128)(2,1)S(1)} %shard_map.94.own_ref), channel_id=1, source_target_pairs={{0,1},{1,0},{2,3},{3,2},{4,5},{5,4},{6,7},{7,6},{8,9},{9,8},{10,11... | collective-permute-start | bytes 393224 | tf_op jit(solution)/shard_map/ppermute | solution.py:759
  99.6 8.1 %collective-permute-start.30 = (bf16[64,1024]{1,0:T(8,128)(2,1)S(1)}, bf16[64,1024]{1,0:T(8,128)(2,1)S(1)}, u32[]{:S(2)}, u32[]{:S(2)}) collective-permute-start(bf16[64,1024]{1,0:T(8,128)(2,1)S(1)} %shard_map.98.own_ref), channel_id=1, source_target_pairs={{0,1},{1,0},{2,3},{3,2},{4,5},{5,4},{6,7},{7,6},{8,9},{9,8},{10,11... | collective-permute-start | bytes 393224 | tf_op jit(solution)/shard_map/ppermute | solution.py:759
  102.6 10.0 %collective-permute-start.19 = (bf16[64,2048]{1,0:T(8,128)(2,1)S(1)}, bf16[64,2048]{1,0:T(8,128)(2,1)S(1)}, u32[]{:S(2)}, u32[]{:S(2)}) collective-permute-start(bf16[64,2048]{1,0:T(8,128)(2,1)S(1)} %get-tuple-element.550), channel_id=1, source_target_pairs={{0,2},{1,3},{2,0},{3,1},{4,6},{5,7},{6,4},{7,5},{8,10},{9,11},{10,... | collective-permute-start | bytes 786440 | tf_op jit(solution)/shard_map/ppermute | solution.py:759
  107.6 8.3 %collective-permute-start.27 = (bf16[64,2048]{1,0:T(8,128)(2,1)S(1)}, bf16[64,2048]{1,0:T(8,128)(2,1)S(1)}, u32[]{:S(2)}, u32[]{:S(2)}) collective-permute-start(bf16[64,2048]{1,0:T(8,128)(2,1)S(1)} %get-tuple-element.564), channel_id=1, source_target_pairs={{0,2},{1,3},{2,0},{3,1},{4,6},{5,7},{6,4},{7,5},{8,10},{9,11},{10,... | collective-permute-start | bytes 786440 | tf_op jit(solution)/shard_map/ppermute | solution.py:759
  107.7 11.0 %collective-permute-start.31 = (bf16[64,2048]{1,0:T(8,128)(2,1)S(1)}, bf16[64,2048]{1,0:T(8,128)(2,1)S(1)}, u32[]{:S(2)}, u32[]{:S(2)}) collective-permute-start(bf16[64,2048]{1,0:T(8,128)(2,1)S(1)} %get-tuple-element.572), channel_id=1, source_target_pairs={{0,2},{1,3},{2,0},{3,1},{4,6},{5,7},{6,4},{7,5},{8,10},{9,11},{10,... | collective-permute-start | bytes 786440 | tf_op jit(solution)/shard_map/ppermute | solution.py:759
where the time goes:
time: 121 us
  Pallas kernels  44.3 us (37%)
  starting transfers between devices  39 us (32%)
  waiting for transfers between devices  36 us (30%)
    pallas_call x26, Pallas kernels, call(): pl.pallas_call(kernel, in_specs=in_specs, out_specs=[IN_VMEM] * len(outs)...  44.3 us
    ppermute x26, starting transfers between devices, send(): return lax.ppermute(value, 'section', pairs)  39 us
    ppermute x26, waiting for transfers between devices, send(): return lax.ppermute(value, 'section', pairs)  36 us
  transfers between devices with their start and end apart: 26, of which 9 were waited for; matrix products, arithmetic and copies ran while one was open for 0% of the time, Pallas kernels for 29%

commit v1 on v0

--- a/solution.py
+++ b/solution.py
@@ -178,8 +178,6 @@
     return kept
 
 
-UNROLL = 1
-AHEAD = 4
 LIMIT = 6 * 1024 * 1024
 CHUNKS = ((0, 2), (4, 6), (1, 3), (5, 7))
 IN_VMEM = pl.BlockSpec(memory_space=pltpu.VMEM)
@@ -360,16 +358,16 @@
     acc_ref, sq_ref = refs
     _, shard = seat()
     features = w_ref.shape[0]
-    pieces = 8 if load == "first" else 2
+    pieces = 4 if load == "first" else 2
     depth = features // pieces
 
     def fetch(i):
-        rows = pl.ds(pl.multiple_of(i * depth, depth), depth)
+        rows = pl.ds(i * depth, depth)
         return pltpu.make_async_copy(w_ref.at[rows], held_ref.at[rows], sem.at[i])
 
     copies = []
     if load == "first":
-        for i in range(AHEAD):
+        for i in range(pieces):
             fetch(i).start()
     elif load == "second":
         copies = [pltpu.make_async_copy(other_ref, held_ref, sem.at[0])]
@@ -380,7 +378,7 @@
         tall = len(CHUNKS[chunk]) * BLOCK
 
         def each(i, carry):
-            columns = pl.ds(pl.multiple_of(i * depth, depth), depth)
+            columns = pl.ds(i * depth if load == "first" else pl.multiple_of(i * depth, depth), depth)
             if kind != "all":
                 base = tall // 2 if kind == "rest" else 0
                 restore = restore_ref[chunk][:tall, base : base + tall // 2]
@@ -394,11 +392,6 @@
             scaled = (x * gain_ref[:, columns].astype(jnp.float32)).astype(jnp.bfloat16)
             if load == "first":
                 fetch(i).wait()
-
-                @pl.when(i + AHEAD < pieces)
-                def _():
-                    fetch(i + AHEAD).start()
-
                 weight = held_ref[columns, :]
             else:
                 weight = w_ref[columns, :]
@@ -409,7 +402,11 @@
 
         acc_ref[:tall, :] = jnp.zeros((tall, acc_ref.shape[1]), jnp.float32)
         sq_ref[:tall, :] = jnp.zeros((tall, sq_ref.shape[1]), jnp.float32)
-        lax.fori_loop(0, pieces, each, 0)
+        if load == "first":
+            for i in range(pieces):
+                each(i, 0)
+        else:
+            lax.fori_loop(0, pieces, each, 0)
         half = BLOCK // 2
         width = keep_ref.shape[1]
         for piece in range(tall // BLOCK):
@@ -559,7 +556,7 @@
     )[0]
 
 
-def output_kernel(jobs, own_ref, recv_ref, active_ref, order_ref, *refs):
+def output_kernel(jobs, sides, own_ref, recv_ref, active_ref, order_ref, *refs):
     refs = list(refs)
     x_refs = [refs.pop(0) for _ in jobs]
     carry_ref = refs.pop(0) if jobs[-1][0] else None
@@ -597,7 +594,7 @@
                 rest_ref[:, inner] = ordered[kept:].astype(jnp.bfloat16)
             return carry
 
-        lax.fori_loop(0, middle // tile, each, 0, unroll=UNROLL)
+        lax.fori_loop(0, middle // tile, each, 0)
 
     def pooled(chunk, kind, x_ref, *outs):
         kept = x_ref.shape[0]
@@ -611,24 +608,24 @@
 
         def each(i, carry):
             inner = pl.ds(pl.multiple_of(i * tile, tile), tile)
-            for side in range(2):
+            for place, side in enumerate(sides):
                 columns = pl.ds(pl.multiple_of(i * tile + side * middle, tile), tile)
                 state = updated(chunk, x_ref, att_ref[:tall, :], columns, base)
-                if len(outs) == 1:
+                if len(outs) < len(sides):
                     outs[0][:, columns] = state
                 else:
-                    outs[side][:, inner] = state
+                    outs[place][:, inner] = state
             return carry
 
-        lax.fori_loop(0, middle // tile, each, 0, unroll=UNROLL)
+        lax.fori_loop(0, middle // tile, each, 0, unroll=2 if len(sides) == 1 else 1)
 
     for (layer, chunk, kind), x_ref in zip(jobs, x_refs):
-        outs = [refs.pop(0) for _ in range(len(result_shapes(layer, chunk, kind, 2 * middle)))]
+        outs = [refs.pop(0) for _ in range(len(result_shapes(layer, chunk, kind, 2 * middle, sides)))]
         if kind == "all":
             on_layer(layer, functools.partial(lower, chunk, x_ref, *outs))
         else:
             on_layer(layer, functools.partial(pooled, chunk, kind, x_ref, *outs))
-        if layer:
+        if layer and 0 in sides:
             swap_ref = outs[0]
 
             def ship():
@@ -637,23 +634,23 @@
             on_layer(0, ship)
 
 
-def result_shapes(layer, chunk, kind, features):
+def result_shapes(layer, chunk, kind, features, sides):
     kept = kept_rows(chunk)
     whole = pltpu.VMEM((kept, features), jnp.bfloat16)
     part = pltpu.VMEM((kept, features // 2), jnp.bfloat16)
     if layer or kind == "rest":
-        return [part, part]
+        return [part] * len(sides)
     return [whole, part, part] if kind == "all" else [whole]
 
 
-def output(jobs, own, recv, active, order, xs, carry, w):
+def output(jobs, own, recv, active, order, xs, carry, w, sides=(0, 1)):
     depth, features = w.shape
     outs = []
     for job in jobs:
-        outs += result_shapes(*job, features)
+        outs += result_shapes(*job, features, sides)
     inputs = [own, recv, active, order, *xs] + [carry] * jobs[-1][0] + [w]
     return call(
-        functools.partial(output_kernel, jobs), inputs, [IN_VMEM] * len(inputs), outs,
+        functools.partial(output_kernel, jobs, sides), inputs, [IN_VMEM] * len(inputs), outs,
         scratch=[pltpu.VMEM((widest(jobs), depth), jnp.bfloat16)],
         flops=2 * widest(jobs) * features * depth,
     )
@@ -774,7 +771,12 @@
         own = attend(jobs, total_width, keep, keep_sq, received, held_cache, limits, query_width)
         other = send(own, swap)
         carry = high_rests[at - LAG] if at >= LAG else None
-        results = list(output(jobs, own, other, active, order, xs, carry, held_out))
+        sides = ((0,), (1,)) if at == count + LAG - 1 else ((0, 1),)
+        results = []
+        for chosen in sides:
+            results += output(
+                jobs, own, other, active, order, xs, carry, held_out, chosen
+            )
         for layer, chunk, kind in jobs:
             if layer:
                 settled.append(send(results.pop(0), across))

time: 121 us -> 120 us (level)
    pallas_call x26 -> x27, Pallas kernels: 44.3 us -> 43.8 us  [call(): pl.pallas_call(kernel, in_specs=in_specs, out_specs=[IN_VMEM] * len(outs)...]
  transfers between devices with their start and end apart: 26 -> 26, of which waited for: 9 -> 10; matrix products, arithmetic and copies ran while one was open for 0% -> 0% of each run, Pallas kernels for 29% -> 29%
where the time goes in v1:
time: 120 us
  Pallas kernels  43.8 us (36%)
  starting transfers between devices  38.2 us (32%)
  waiting for transfers between devices  36.8 us (31%)
  between operations  1.2 us (1%)
    pallas_call x27, Pallas kernels, call(): pl.pallas_call(kernel, in_specs=in_specs, out_specs=[IN_VMEM] * len(outs)...  43.8 us
    ppermute x26, starting transfers between devices, send(): return lax.ppermute(value, 'section', pairs)  38.2 us
    ppermute x26, waiting for transfers between devices, send(): return lax.ppermute(value, 'section', pairs)  36.8 us
  transfers between devices with their start and end apart: 26, of which 10 were waited for; matrix products, arithmetic and copies ran while one was open for 0% of the time, Pallas kernels for 29%

profile of v1, /device:TPU:0, one launch (start us, length us, event | category | flops | bytes accessed | tf_op | source)
XLA Modules:
  0.0 120.1 jit_solution(9718465836405585934)
XLA Ops:
  0.0 6.5 %shard_map.77 = (f32[64,1280]{1,0:T(8,128)S(1)}, f32[64,128]{1,0:T(8,128)S(1)}, bf16[64,1408]{1,0:T(8,128)(2,1)S(1)}, bf16[4096,1280]{1,0:T(8,128)(2,1)S(1)}, bf16[128,4096]{1,0:T(8,128)(2,1)S(1)}) custom-call(bf16[256,4096]{1,0:T(8,128)(2,1)} %bitcast.42, bf16[1,4096]{1,0:T(2,128)(2,1)} %refs_2_.3, bf16[4096,1280]{1,0:T(8,128)(2,1)} %bitcast.36), custom_call_target="tpu_custom_call" | custom-call | flops 1342177280 | bytes 1000000 | tf_op jit(solution)/shard_map/pallas_call | solution.py:189
  6.5 3.0 %collective-permute-start.7 = (bf16[64,1408]{1,0:T(8,128)(2,1)S(1)}, bf16[64,1408]{1,0:T(8,128)(2,1)S(1)}, u32[]{:S(2)}, u32[]{:S(2)}) collective-permute-start(bf16[64,1408]{1,0:T(8,128)(2,1)S(1)} %get-tuple-element.523), channel_id=1, source_target_pairs={{0,1},{1,0},{2,3},{3,2},{4,5},{5,4},{6,7},{7,6},{8,9},{9,8},{10,11... | collective-permute-start | bytes 540680 | tf_op jit(solution)/shard_map/ppermute | solution.py:756
  9.6 1.4 %shard_map.75 = (bf16[4,128,128]{2,1,0:T(8,128)(2,1)S(1)}, bf16[4,128,128]{2,1,0:T(8,128)(2,1)S(1)}, f32[4,128,128]{2,1,0:T(8,128)S(1)}, f32[2,8,512]{2,1,0:T(8,128)S(1)}, s32[1]{0:T(128)}) custom-call(s32[4,128]{1,0:T(4,128)} %bitcast.55, s32[4,128]{1,0:T(4,128)S(1)} %bitcast.56), custom_call_target="tpu_custom_call" | custom-call | flops 100000000 | bytes 1000000 | tf_op jit(solution)/shard_map/pallas_call | solution.py:189
  11.3 2.8 %collective-permute-done.7.refs_2_ = bf16[64,1408]{1,0:T(8,128)(2,1)S(1)} collective-permute-done((bf16[64,1408]{1,0:T(8,128)(2,1)S(1)}, bf16[64,1408]{1,0:T(8,128)(2,1)S(1)}, u32[]{:S(2)}, u32[]{:S(2)}) %collective-permute-start.7) | collective-permute-done | bytes 180256 | tf_op jit(solution)/shard_map/ppermute | solution.py:756
  14.8 1.8 %collective-permute-start.8 = (bf16[64,1024]{1,0:T(8,128)(2,1)S(1)}, bf16[64,1024]{1,0:T(8,128)(2,1)S(1)}, u32[]{:S(2)}, u32[]{:S(2)}) collective-permute-start(bf16[64,1024]{1,0:T(8,128)(2,1)S(1)} %shard_map.78.own_ref), channel_id=1, source_target_pairs={{0,1},{1,0},{2,3},{3,2},{4,5},{5,4},{6,7},{7,6},{8,9},{9,8},{10,11... | collective-permute-start | bytes 393224 | tf_op jit(solution)/shard_map/ppermute | solution.py:756
  19.2 2.6 %shard_map.79 = (f32[64,1280]{1,0:T(8,128)S(1)}, f32[64,128]{1,0:T(8,128)S(1)}, bf16[64,1408]{1,0:T(8,128)(2,1)S(1)}, bf16[1024,4096]{1,0:T(8,128)(2,1)S(1)}) custom-call(bf16[128,4096]{1,0:T(8,128)(2,1)S(1)} %get-tuple-element.528.refs_0_, bf16[1,4096]{1,0:T(2,128)(2,1)S(1)} %copy-done.4, bf16[4096,1280]{1,0:T(8,128)(2,1)S(1)} %get-tuple-element.529.refs_2_.refs_4_.refs_3_, ...), custom_call_target="tpu_custom_call" | custom-call | flops 1342177280 | bytes 1000000 | tf_op jit(solution)/shard_map/pallas_call | solution.py:189
  21.8 3.2 %shard_map.80 = (bf16[64,4096]{1,0:T(8,128)(2,1)S(1)}, bf16[64,2048]{1,0:T(8,128)(2,1)S(1)}, bf16[64,2048]{1,0:T(8,128)(2,1)S(1)}) custom-call(bf16[64,1024]{1,0:T(8,128)(2,1)S(1)} %shard_map.78.own_ref, bf16[64,1024]{1,0:T(8,128)(2,1)S(1)} %collective-permute-done.8.recv_ref, f32[4,128,128]{2,1,0:T(8,128)S(1)} %get-tuple-element.526.active_ref, ...), custom_call_target="tpu_custom_call" | custom-call | flops 1073741824 | bytes 1000000 | tf_op jit(solution)/shard_map/pallas_call | solution.py:189
  25.1 1.3 %collective-permute-start.9 = (bf16[64,4096]{1,0:T(8,128)(2,1)S(1)}, bf16[64,4096]{1,0:T(8,128)(2,1)S(1)}, u32[]{:S(2)}, u32[]{:S(2)}) collective-permute-start(bf16[64,4096]{1,0:T(8,128)(2,1)S(1)} %get-tuple-element.531), channel_id=1, source_target_pairs={{0,2},{1,3},{4,6},{5,7},{8,10},{9,11},{12,14},{13,15},{16,18},{17,... | collective-permute-start | bytes 1572872 | tf_op jit(solution)/shard_map/ppermute | solution.py:756
  28.0 16.5 %collective-permute-done.21.refs_0_ = bf16[64,4096]{1,0:T(8,128)(2,1)S(1)} collective-permute-done((bf16[64,4096]{1,0:T(8,128)(2,1)S(1)}, bf16[64,4096]{1,0:T(8,128)(2,1)S(1)}, u32[]{:S(2)}, u32[]{:S(2)}) %collective-permute-start.21) | collective-permute-done | bytes 524320 | tf_op jit(solution)/shard_map/ppermute | solution.py:756
  44.5 2.4 %shard_map.90 = (f32[64,1280]{1,0:T(8,128)S(1)}, f32[64,128]{1,0:T(8,128)S(1)}, bf16[64,1408]{1,0:T(8,128)(2,1)S(1)}) custom-call(bf16[64,4096]{1,0:T(8,128)(2,1)S(1)} %collective-permute-done.21.refs_0_, bf16[4,128,128]{2,1,0:T(8,128)(2,1)S(1)} %get-tuple-element.518.refs_2_.restore_ref.refs_1_, bf16[1,4096]{1,0:T(2,128)(2,1)S(1)} %copy-done.4, ...), custom_call_target="tpu_custom_call" | custom-call | flops 1342177280 | bytes 1000000 | tf_op jit(solution)/shard_map/pallas_call | solution.py:189
  48.0 1.8 %collective-permute-start.15 = (bf16[64,1024]{1,0:T(8,128)(2,1)S(1)}, bf16[64,1024]{1,0:T(8,128)(2,1)S(1)}, u32[]{:S(2)}, u32[]{:S(2)}) collective-permute-start(bf16[64,1024]{1,0:T(8,128)(2,1)S(1)} %shard_map.84.own_ref), channel_id=1, source_target_pairs={{0,1},{1,0},{2,3},{3,2},{4,5},{5,4},{6,7},{7,6},{8,9},{9,8},{10,11... | collective-permute-start | bytes 393224 | tf_op jit(solution)/shard_map/ppermute | solution.py:756
  49.8 2.4 %shard_map.81 = (f32[64,1280]{1,0:T(8,128)S(1)}, f32[64,128]{1,0:T(8,128)S(1)}, bf16[64,1408]{1,0:T(8,128)(2,1)S(1)}) custom-call(bf16[64,4096]{1,0:T(8,128)(2,1)S(1)} %collective-permute-done.6.refs_0_, bf16[64,4096]{1,0:T(8,128)(2,1)S(1)} %collective-permute-done.9.refs_1_, bf16[4,128,128]{2,1,0:T(8,128)(2,1)S(1)} %get-tuple-element.518.refs_2_.restore_ref.refs_1_, ...), custom_call_target="tpu_custom_call" | custom-call | flops 1342177280 | bytes 1000000 | tf_op jit(solution)/shard_map/pallas_call | solution.py:189
  52.5 1.9 %collective-permute-done.22.refs_2_ = bf16[64,1408]{1,0:T(8,128)(2,1)S(1)} collective-permute-done((bf16[64,1408]{1,0:T(8,128)(2,1)S(1)}, bf16[64,1408]{1,0:T(8,128)(2,1)S(1)}, u32[]{:S(2)}, u32[]{:S(2)}) %collective-permute-start.22) | collective-permute-done | bytes 180256 | tf_op jit(solution)/shard_map/ppermute | solution.py:756
  56.5 3.2 %shard_map.85 = (bf16[64,4096]{1,0:T(8,128)(2,1)S(1)}, bf16[64,2048]{1,0:T(8,128)(2,1)S(1)}, bf16[64,2048]{1,0:T(8,128)(2,1)S(1)}) custom-call(bf16[64,1024]{1,0:T(8,128)(2,1)S(1)} %shard_map.84.own_ref, bf16[64,1024]{1,0:T(8,128)(2,1)S(1)} %collective-permute-done.15.recv_ref, f32[4,128,128]{2,1,0:T(8,128)S(1)} %get-tuple-element.526.active_ref, ...), custom_call_target="tpu_custom_call" | custom-call | flops 1073741824 | bytes 1000000 | tf_op jit(solution)/shard_map/pallas_call | solution.py:189
  62.7 1.5 %collective-permute-start.20 = (bf16[64,4096]{1,0:T(8,128)(2,1)S(1)}, bf16[64,4096]{1,0:T(8,128)(2,1)S(1)}, u32[]{:S(2)}, u32[]{:S(2)}) collective-permute-start(bf16[64,4096]{1,0:T(8,128)(2,1)S(1)} %get-tuple-element.553), channel_id=1, source_target_pairs={{2,0},{3,1},{6,4},{7,5},{10,8},{11,9},{14,12},{15,13},{18,16},{19,... | collective-permute-start | bytes 1572872 | tf_op jit(solution)/shard_map/ppermute | solution.py:756
  64.2 2.2 %shard_map.92 = bf16[64,4096]{1,0:T(8,128)(2,1)S(1)} custom-call(bf16[64,1024]{1,0:T(8,128)(2,1)S(1)} %shard_map.91.own_ref, bf16[64,1024]{1,0:T(8,128)(2,1)S(1)} %collective-permute-done.23.recv_ref, f32[4,128,128]{2,1,0:T(8,128)S(1)} %get-tuple-element.526.active_ref, bf16[4,128,128]{2,1,0:T(8,128)(2,1)S(1)} %get-tuple-element.519.order_ref, ...), custom_call_target="tpu_custom_call" | custom-call | flops 1073741824 | bytes 1000000 | tf_op jit(solution)/shard_map/pallas_call | solution.py:189
  66.3 2.5 %collective-permute-start.24 = (bf16[64,4096]{1,0:T(8,128)(2,1)S(1)}, bf16[64,4096]{1,0:T(8,128)(2,1)S(1)}, u32[]{:S(2)}, u32[]{:S(2)}) collective-permute-start(bf16[64,4096]{1,0:T(8,128)(2,1)S(1)} %shard_map.92), channel_id=1, source_target_pairs={{0,2},{1,3},{4,6},{5,7},{8,10},{9,11},{12,14},{13,15},{16,18},{17,... | collective-permute-start | bytes 1572872 | tf_op jit(solution)/shard_map/ppermute | solution.py:756
  68.8 2.2 %shard_map.83 = (bf16[64,4096]{1,0:T(8,128)(2,1)S(1)}, bf16[64,2048]{1,0:T(8,128)(2,1)S(1)}, bf16[64,2048]{1,0:T(8,128)(2,1)S(1)}) custom-call(bf16[64,1024]{1,0:T(8,128)(2,1)S(1)} %shard_map.82.own_ref, bf16[64,1024]{1,0:T(8,128)(2,1)S(1)} %collective-permute-done.11.recv_ref, f32[4,128,128]{2,1,0:T(8,128)S(1)} %get-tuple-element.526.active_ref, ...), custom_call_target="tpu_custom_call" | custom-call | flops 1073741824 | bytes 1000000 | tf_op jit(solution)/shard_map/pallas_call | solution.py:189
  71.0 1.3 %collective-permute-start.28 = (bf16[64,4096]{1,0:T(8,128)(2,1)S(1)}, bf16[64,4096]{1,0:T(8,128)(2,1)S(1)}, u32[]{:S(2)}, u32[]{:S(2)}) collective-permute-start(bf16[64,4096]{1,0:T(8,128)(2,1)S(1)} %get-tuple-element.565), channel_id=1, source_target_pairs={{0,2},{1,3},{4,6},{5,7},{8,10},{9,11},{12,14},{13,15},{16,18},{17,... | collective-permute-start | bytes 1572872 | tf_op jit(solution)/shard_map/ppermute | solution.py:756
  73.3 2.5 %shard_map.86 = (f32[64,1280]{1,0:T(8,128)S(1)}, f32[64,128]{1,0:T(8,128)S(1)}, bf16[64,1408]{1,0:T(8,128)(2,1)S(1)}) custom-call(bf16[64,4096]{1,0:T(8,128)(2,1)S(1)} %collective-permute-done.13.refs_0_, bf16[64,4096]{1,0:T(8,128)(2,1)S(1)} %collective-permute-done.16.refs_1_, bf16[4,128,128]{2,1,0:T(8,128)(2,1)S(1)} %get-tuple-element.518.refs_2_.restore_ref.refs_1_, ...), custom_call_target="tpu_custom_call" | custom-call | flops 1342177280 | bytes 1000000 | tf_op jit(solution)/shard_map/pallas_call | solution.py:189
  76.8 7.0 %collective-permute-done.24.refs_1_ = bf16[64,4096]{1,0:T(8,128)(2,1)S(1)} collective-permute-done((bf16[64,4096]{1,0:T(8,128)(2,1)S(1)}, bf16[64,4096]{1,0:T(8,128)(2,1)S(1)}, u32[]{:S(2)}, u32[]{:S(2)}) %collective-permute-start.24) | collective-permute-done | bytes 524320 | tf_op jit(solution)/shard_map/ppermute | solution.py:756
  83.8 2.5 %shard_map.93 = (f32[64,1280]{1,0:T(8,128)S(1)}, f32[64,128]{1,0:T(8,128)S(1)}, bf16[64,1408]{1,0:T(8,128)(2,1)S(1)}) custom-call(bf16[64,4096]{1,0:T(8,128)(2,1)S(1)} %collective-permute-done.20.refs_0_, bf16[64,4096]{1,0:T(8,128)(2,1)S(1)} %collective-permute-done.24.refs_1_, bf16[4,128,128]{2,1,0:T(8,128)(2,1)S(1)} %get-tuple-element.518.refs_2_.restore_ref.refs_1_, ...), custom_call_target="tpu_custom_call" | custom-call | flops 1342177280 | bytes 1000000 | tf_op jit(solution)/shard_map/pallas_call | solution.py:189
  87.5 1.9 %collective-permute-done.28.refs_0_ = bf16[64,4096]{1,0:T(8,128)(2,1)S(1)} collective-permute-done((bf16[64,4096]{1,0:T(8,128)(2,1)S(1)}, bf16[64,4096]{1,0:T(8,128)(2,1)S(1)}, u32[]{:S(2)}, u32[]{:S(2)}) %collective-permute-start.28) | collective-permute-done | bytes 524320 | tf_op jit(solution)/shard_map/ppermute | solution.py:756
  92.2 4.9 %collective-permute-start.12 = (bf16[64,2048]{1,0:T(8,128)(2,1)S(1)}, bf16[64,2048]{1,0:T(8,128)(2,1)S(1)}, u32[]{:S(2)}, u32[]{:S(2)}) collective-permute-start(bf16[64,2048]{1,0:T(8,128)(2,1)S(1)} %get-tuple-element.536), channel_id=1, source_target_pairs={{0,2},{1,3},{2,0},{3,1},{4,6},{5,7},{6,4},{7,5},{8,10},{9,11},{10,... | collective-permute-start | bytes 786440 | tf_op jit(solution)/shard_map/ppermute | solution.py:756
  99.9 2.2 %shard_map.88 = (bf16[64,2048]{1,0:T(8,128)(2,1)S(1)}, bf16[64,2048]{1,0:T(8,128)(2,1)S(1)}, bf16[64,2048]{1,0:T(8,128)(2,1)S(1)}, bf16[64,2048]{1,0:T(8,128)(2,1)S(1)}) custom-call(bf16[64,1024]{1,0:T(8,128)(2,1)S(1)} %shard_map.87.own_ref, bf16[64,1024]{1,0:T(8,128)(2,1)S(1)} %collective-permute-done.18.recv_ref, ...), custom_call_target="tpu_custom_call" | custom-call | flops 1073741824 | bytes 1000000 | tf_op jit(solution)/shard_map/pallas_call | solution.py:189
  102.1 3.0 %collective-permute-start.19 = (bf16[64,2048]{1,0:T(8,128)(2,1)S(1)}, bf16[64,2048]{1,0:T(8,128)(2,1)S(1)}, u32[]{:S(2)}, u32[]{:S(2)}) collective-permute-start(bf16[64,2048]{1,0:T(8,128)(2,1)S(1)} %get-tuple-element.548), channel_id=1, source_target_pairs={{0,2},{1,3},{2,0},{3,1},{4,6},{5,7},{6,4},{7,5},{8,10},{9,11},{10,... | collective-permute-start | bytes 786440 | tf_op jit(solution)/shard_map/ppermute | solution.py:756
  105.1 2.4 %shard_map.95 = (bf16[64,2048]{1,0:T(8,128)(2,1)S(1)}, bf16[64,2048]{1,0:T(8,128)(2,1)S(1)}, bf16[64,2048]{1,0:T(8,128)(2,1)S(1)}, bf16[64,2048]{1,0:T(8,128)(2,1)S(1)}) custom-call(bf16[64,1024]{1,0:T(8,128)(2,1)S(1)} %shard_map.94.own_ref, bf16[64,1024]{1,0:T(8,128)(2,1)S(1)} %collective-permute-done.26.recv_ref, ...), custom_call_target="tpu_custom_call" | custom-call | flops 1073741824 | bytes 1000000 | tf_op jit(solution)/shard_map/pallas_call | solution.py:189
  107.6 3.2 %collective-permute-start.31 = (bf16[64,2048]{1,0:T(8,128)(2,1)S(1)}, bf16[64,2048]{1,0:T(8,128)(2,1)S(1)}, u32[]{:S(2)}, u32[]{:S(2)}) collective-permute-start(bf16[64,2048]{1,0:T(8,128)(2,1)S(1)} %shard_map.99), channel_id=1, source_target_pairs={{0,2},{1,3},{2,0},{3,1},{4,6},{5,7},{6,4},{7,5},{8,10},{9,11},{10,... | collective-permute-start | bytes 786440 | tf_op jit(solution)/shard_map/ppermute | solution.py:756
  112.2 1.4 %shard_map.89 = (bf16[128,2048]{1,0:T(8,128)(2,1)S(1)}, bf16[128,2048]{1,0:T(8,128)(2,1)S(1)}) custom-call(bf16[4,128,128]{2,1,0:T(8,128)(2,1)S(1)} %get-tuple-element.518.refs_2_.restore_ref.refs_1_, bf16[64,2048]{1,0:T(8,128)(2,1)S(1)} %collective-permute-done.12.refs_0_, bf16[64,2048]{1,0:T(8,128)(2,1)S(1)} %get-tuple-element.537.refs_1_, ...), custom_call_target="tpu_custom_call" | custom-call | flops 100000000 | bytes 1000000 | tf_op jit(solution)/shard_map/pallas_call | solution.py:189
  113.7 1.8 %collective-permute-done.27.refs_0_ = bf16[64,2048]{1,0:T(8,128)(2,1)S(1)} collective-permute-done((bf16[64,2048]{1,0:T(8,128)(2,1)S(1)}, bf16[64,2048]{1,0:T(8,128)(2,1)S(1)}, u32[]{:S(2)}, u32[]{:S(2)}) %collective-permute-start.27) | collective-permute-done | bytes 262176 | tf_op jit(solution)/shard_map/ppermute | solution.py:756
  116.2 2.1 %collective-permute-done.31.refs_3_ = bf16[64,2048]{1,0:T(8,128)(2,1)S(1)} collective-permute-done((bf16[64,2048]{1,0:T(8,128)(2,1)S(1)}, bf16[64,2048]{1,0:T(8,128)(2,1)S(1)}, u32[]{:S(2)}, u32[]{:S(2)}) %collective-permute-start.31) | collective-permute-done | bytes 262176 | tf_op jit(solution)/shard_map/ppermute | solution.py:756
  118.3 1.6 %shard_map.101 = bf16[512,2048]{1,0:T(8,128)(2,1)} custom-call(bf16[4,128,128]{2,1,0:T(8,128)(2,1)S(1)} %get-tuple-element.518.refs_2_.restore_ref.refs_1_, bf16[128,2048]{1,0:T(8,128)(2,1)S(1)} %get-tuple-element.551.refs_0_, bf16[128,2048]{1,0:T(8,128)(2,1)S(1)} %get-tuple-element.552.refs_1_, bf16[128,2048]{1,0:T(8,128)(2,1)S(1)} %shard_map.96.refs_2_, ...), custom_call_target="tpu_custom_call" | custom-call | flops 100000000 | bytes 1000000 | tf_op jit(solution)/shard_map/pallas_call | solution.py:189
  (61 shorter events, 21.8 us)
Async XLA Ops:
  0.0 19.2 %slice-start = ((s8[8388608]{0:T(1024)(128)(4,1)}), s8[4194304]{0:T(1024)(128)(4,1)S(1)}, s32[]{:S(2)}) async-start(s8[8388608]{0:T(1024)(128)(4,1)} %bitcast.38), calls=%async_computation | async-start | bytes 8388608
  0.0 9.6 %copy-start.8 = (s32[512]{0:T(512)S(1)}, s32[512]{0:T(512)}, u32[]{:S(2)}) copy-start(s32[512]{0:T(512)} %param.19) | copy-start | bytes 6148
  0.0 11.0 %copy-start = (bf16[1,256,4096]{2,1,0:T(8,128)(2,1)S(1)}, bf16[1,256,4096]{2,1,0:T(8,128)(2,1)}, u32[]{:S(2)}) copy-start(bf16[1,256,4096]{2,1,0:T(8,128)(2,1)} %param.17) | copy-start | bytes 6291460
  0.0 11.0 %copy-start.3 = (bf16[1,256,16,256]{3,2,1,0:T(8,128)(2,1)S(1)}, bf16[1,256,16,256]{3,2,1,0:T(8,128)(2,1)}, u32[]{:S(2)}) copy-start(bf16[1,256,16,256]{3,2,1,0:T(8,128)(2,1)} %param.20) | copy-start | bytes 6291460
  0.0 19.2 %slice-start.1 = ((s8[8388608]{0:T(1024)(128)(4,1)}), s8[4194304]{0:T(1024)(128)(4,1)S(1)}, s32[]{:S(2)}) async-start(s8[8388608]{0:T(1024)(128)(4,1)} %bitcast.38), calls=%async_computation.1 | async-start | bytes 8388608
  6.5 7.6 %collective-permute-start.7 = (bf16[64,1408]{1,0:T(8,128)(2,1)S(1)}, bf16[64,1408]{1,0:T(8,128)(2,1)S(1)}, u32[]{:S(2)}, u32[]{:S(2)}) collective-permute-start(bf16[64,1408]{1,0:T(8,128)(2,1)S(1)} %get-tuple-element.523), channel_id=1, source_target_pairs={{0,1},{1,0},{2,3},{3,2},{4,5},{5,4},{6,7},{7,6},{8,9},{9,8},{10,11... | collective-permute-start | bytes 540680 | tf_op jit(solution)/shard_map/ppermute | solution.py:756
  11.3 8.0 %copy-start.4 = (bf16[1,4096]{1,0:T(2,128)(2,1)S(1)}, bf16[1,4096]{1,0:T(2,128)(2,1)}, u32[]{:S(2)}) copy-start(bf16[1,4096]{1,0:T(2,128)(2,1)} %refs_2_.3) | copy-start | bytes 24580
  14.8 7.0 %collective-permute-start.8 = (bf16[64,1024]{1,0:T(8,128)(2,1)S(1)}, bf16[64,1024]{1,0:T(8,128)(2,1)S(1)}, u32[]{:S(2)}, u32[]{:S(2)}) collective-permute-start(bf16[64,1024]{1,0:T(8,128)(2,1)S(1)} %shard_map.78.own_ref), channel_id=1, source_target_pairs={{0,1},{1,0},{2,3},{3,2},{4,5},{5,4},{6,7},{7,6},{8,9},{9,8},{10,11... | collective-permute-start | bytes 393224 | tf_op jit(solution)/shard_map/ppermute | solution.py:756
  16.6 33.2 %collective-permute-start.6 = (bf16[64,4096]{1,0:T(8,128)(2,1)S(1)}, bf16[64,4096]{1,0:T(8,128)(2,1)S(1)}, u32[]{:S(2)}, u32[]{:S(2)}) collective-permute-start(bf16[64,4096]{1,0:T(8,128)(2,1)S(1)} %get-tuple-element.520), channel_id=1, source_target_pairs={{2,0},{3,1},{6,4},{7,5},{10,8},{11,9},{14,12},{15,13},{18,16},{19,... | collective-permute-start | bytes 1572872 | tf_op jit(solution)/shard_map/ppermute | solution.py:756
  17.9 26.6 %collective-permute-start.21 = (bf16[64,4096]{1,0:T(8,128)(2,1)S(1)}, bf16[64,4096]{1,0:T(8,128)(2,1)S(1)}, u32[]{:S(2)}, u32[]{:S(2)}) collective-permute-start(bf16[64,4096]{1,0:T(8,128)(2,1)S(1)} %get-tuple-element.554), channel_id=1, source_target_pairs={{2,0},{3,1},{6,4},{7,5},{10,8},{11,9},{14,12},{15,13},{18,16},{19,... | collective-permute-start | bytes 1572872 | tf_op jit(solution)/shard_map/ppermute | solution.py:756
  25.1 24.7 %collective-permute-start.9 = (bf16[64,4096]{1,0:T(8,128)(2,1)S(1)}, bf16[64,4096]{1,0:T(8,128)(2,1)S(1)}, u32[]{:S(2)}, u32[]{:S(2)}) collective-permute-start(bf16[64,4096]{1,0:T(8,128)(2,1)S(1)} %get-tuple-element.531), channel_id=1, source_target_pairs={{0,2},{1,3},{4,6},{5,7},{8,10},{9,11},{12,14},{13,15},{16,18},{17,... | collective-permute-start | bytes 1572872 | tf_op jit(solution)/shard_map/ppermute | solution.py:756
  26.4 20.9 %collective-permute-start.14 = (bf16[64,1408]{1,0:T(8,128)(2,1)S(1)}, bf16[64,1408]{1,0:T(8,128)(2,1)S(1)}, u32[]{:S(2)}, u32[]{:S(2)}) collective-permute-start(bf16[64,1408]{1,0:T(8,128)(2,1)S(1)} %get-tuple-element.542), channel_id=1, source_target_pairs={{0,1},{1,0},{2,3},{3,2},{4,5},{5,4},{6,7},{7,6},{8,9},{9,8},{10,11... | collective-permute-start | bytes 540680 | tf_op jit(solution)/shard_map/ppermute | solution.py:756
  26.7 45.6 %collective-permute-start.13 = (bf16[64,4096]{1,0:T(8,128)(2,1)S(1)}, bf16[64,4096]{1,0:T(8,128)(2,1)S(1)}, u32[]{:S(2)}, u32[]{:S(2)}) collective-permute-start(bf16[64,4096]{1,0:T(8,128)(2,1)S(1)} %get-tuple-element.539), channel_id=1, source_target_pairs={{2,0},{3,1},{6,4},{7,5},{10,8},{11,9},{14,12},{15,13},{18,16},{19,... | collective-permute-start | bytes 1572872 | tf_op jit(solution)/shard_map/ppermute | solution.py:756
  47.0 7.5 %collective-permute-start.22 = (bf16[64,1408]{1,0:T(8,128)(2,1)S(1)}, bf16[64,1408]{1,0:T(8,128)(2,1)S(1)}, u32[]{:S(2)}, u32[]{:S(2)}) collective-permute-start(bf16[64,1408]{1,0:T(8,128)(2,1)S(1)} %get-tuple-element.557), channel_id=1, source_target_pairs={{0,1},{1,0},{2,3},{3,2},{4,5},{5,4},{6,7},{7,6},{8,9},{9,8},{10,11... | collective-permute-start | bytes 540680 | tf_op jit(solution)/shard_map/ppermute | solution.py:756
  48.0 8.6 %collective-permute-start.15 = (bf16[64,1024]{1,0:T(8,128)(2,1)S(1)}, bf16[64,1024]{1,0:T(8,128)(2,1)S(1)}, u32[]{:S(2)}, u32[]{:S(2)}) collective-permute-start(bf16[64,1024]{1,0:T(8,128)(2,1)S(1)} %shard_map.84.own_ref), channel_id=1, source_target_pairs={{0,1},{1,0},{2,3},{3,2},{4,5},{5,4},{6,7},{7,6},{8,9},{9,8},{10,11... | collective-permute-start | bytes 393224 | tf_op jit(solution)/shard_map/ppermute | solution.py:756
  52.2 8.8 %collective-permute-start.10 = (bf16[64,1408]{1,0:T(8,128)(2,1)S(1)}, bf16[64,1408]{1,0:T(8,128)(2,1)S(1)}, u32[]{:S(2)}, u32[]{:S(2)}) collective-permute-start(bf16[64,1408]{1,0:T(8,128)(2,1)S(1)} %get-tuple-element.534), channel_id=1, source_target_pairs={{0,1},{1,0},{2,3},{3,2},{4,5},{5,4},{6,7},{7,6},{8,9},{9,8},{10,11... | collective-permute-start | bytes 540680 | tf_op jit(solution)/shard_map/ppermute | solution.py:756
  55.1 9.1 %collective-permute-start.23 = (bf16[64,1024]{1,0:T(8,128)(2,1)S(1)}, bf16[64,1024]{1,0:T(8,128)(2,1)S(1)}, u32[]{:S(2)}, u32[]{:S(2)}) collective-permute-start(bf16[64,1024]{1,0:T(8,128)(2,1)S(1)} %shard_map.91.own_ref), channel_id=1, source_target_pairs={{0,1},{1,0},{2,3},{3,2},{4,5},{5,4},{6,7},{7,6},{8,9},{9,8},{10,11... | collective-permute-start | bytes 393224 | tf_op jit(solution)/shard_map/ppermute | solution.py:756
  59.7 13.6 %collective-permute-start.16 = (bf16[64,4096]{1,0:T(8,128)(2,1)S(1)}, bf16[64,4096]{1,0:T(8,128)(2,1)S(1)}, u32[]{:S(2)}, u32[]{:S(2)}) collective-permute-start(bf16[64,4096]{1,0:T(8,128)(2,1)S(1)} %get-tuple-element.543), channel_id=1, source_target_pairs={{0,2},{1,3},{4,6},{5,7},{8,10},{9,11},{12,14},{13,15},{16,18},{17,... | collective-permute-start | bytes 1572872 | tf_op jit(solution)/shard_map/ppermute | solution.py:756
  61.8 7.0 %collective-permute-start.11 = (bf16[64,1024]{1,0:T(8,128)(2,1)S(1)}, bf16[64,1024]{1,0:T(8,128)(2,1)S(1)}, u32[]{:S(2)}, u32[]{:S(2)}) collective-permute-start(bf16[64,1024]{1,0:T(8,128)(2,1)S(1)} %shard_map.82.own_ref), channel_id=1, source_target_pairs={{0,1},{1,0},{2,3},{3,2},{4,5},{5,4},{6,7},{7,6},{8,9},{9,8},{10,11... | collective-permute-start | bytes 393224 | tf_op jit(solution)/shard_map/ppermute | solution.py:756
  62.7 14.1 %collective-permute-start.20 = (bf16[64,4096]{1,0:T(8,128)(2,1)S(1)}, bf16[64,4096]{1,0:T(8,128)(2,1)S(1)}, u32[]{:S(2)}, u32[]{:S(2)}) collective-permute-start(bf16[64,4096]{1,0:T(8,128)(2,1)S(1)} %get-tuple-element.553), channel_id=1, source_target_pairs={{2,0},{3,1},{6,4},{7,5},{10,8},{11,9},{14,12},{15,13},{18,16},{19,... | collective-permute-start | bytes 1572872 | tf_op jit(solution)/shard_map/ppermute | solution.py:756
  66.3 17.4 %collective-permute-start.24 = (bf16[64,4096]{1,0:T(8,128)(2,1)S(1)}, bf16[64,4096]{1,0:T(8,128)(2,1)S(1)}, u32[]{:S(2)}, u32[]{:S(2)}) collective-permute-start(bf16[64,4096]{1,0:T(8,128)(2,1)S(1)} %shard_map.92), channel_id=1, source_target_pairs={{0,2},{1,3},{4,6},{5,7},{8,10},{9,11},{12,14},{13,15},{16,18},{17,... | collective-permute-start | bytes 1572872 | tf_op jit(solution)/shard_map/ppermute | solution.py:756
  71.0 18.4 %collective-permute-start.28 = (bf16[64,4096]{1,0:T(8,128)(2,1)S(1)}, bf16[64,4096]{1,0:T(8,128)(2,1)S(1)}, u32[]{:S(2)}, u32[]{:S(2)}) collective-permute-start(bf16[64,4096]{1,0:T(8,128)(2,1)S(1)} %get-tuple-element.565), channel_id=1, source_target_pairs={{0,2},{1,3},{4,6},{5,7},{8,10},{9,11},{12,14},{13,15},{16,18},{17,... | collective-permute-start | bytes 1572872 | tf_op jit(solution)/shard_map/ppermute | solution.py:756
  75.9 14.7 %collective-permute-start.17 = (bf16[64,1408]{1,0:T(8,128)(2,1)S(1)}, bf16[64,1408]{1,0:T(8,128)(2,1)S(1)}, u32[]{:S(2)}, u32[]{:S(2)}) collective-permute-start(bf16[64,1408]{1,0:T(8,128)(2,1)S(1)} %get-tuple-element.546), channel_id=1, source_target_pairs={{0,1},{1,0},{2,3},{3,2},{4,5},{5,4},{6,7},{7,6},{8,9},{9,8},{10,11... | collective-permute-start | bytes 540680 | tf_op jit(solution)/shard_map/ppermute | solution.py:756
  86.3 10.8 %collective-permute-start.25 = (bf16[64,1408]{1,0:T(8,128)(2,1)S(1)}, bf16[64,1408]{1,0:T(8,128)(2,1)S(1)}, u32[]{:S(2)}, u32[]{:S(2)}) collective-permute-start(bf16[64,1408]{1,0:T(8,128)(2,1)S(1)} %get-tuple-element.560), channel_id=1, source_target_pairs={{0,1},{1,0},{2,3},{3,2},{4,5},{5,4},{6,7},{7,6},{8,9},{9,8},{10,11... | collective-permute-start | bytes 540680 | tf_op jit(solution)/shard_map/ppermute | solution.py:756
  89.4 9.7 %collective-permute-start.29 = (bf16[64,1408]{1,0:T(8,128)(2,1)S(1)}, bf16[64,1408]{1,0:T(8,128)(2,1)S(1)}, u32[]{:S(2)}, u32[]{:S(2)}) collective-permute-start(bf16[64,1408]{1,0:T(8,128)(2,1)S(1)} %get-tuple-element.568), channel_id=1, source_target_pairs={{0,1},{1,0},{2,3},{3,2},{4,5},{5,4},{6,7},{7,6},{8,9},{9,8},{10,11... | collective-permute-start | bytes 540680 | tf_op jit(solution)/shard_map/ppermute | solution.py:756
  91.2 8.7 %collective-permute-start.18 = (bf16[64,1024]{1,0:T(8,128)(2,1)S(1)}, bf16[64,1024]{1,0:T(8,128)(2,1)S(1)}, u32[]{:S(2)}, u32[]{:S(2)}) collective-permute-start(bf16[64,1024]{1,0:T(8,128)(2,1)S(1)} %shard_map.87.own_ref), channel_id=1, source_target_pairs={{0,1},{1,0},{2,3},{3,2},{4,5},{5,4},{6,7},{7,6},{8,9},{9,8},{10,11... | collective-permute-start | bytes 393224 | tf_op jit(solution)/shard_map/ppermute | solution.py:756
  92.2 19.3 %collective-permute-start.12 = (bf16[64,2048]{1,0:T(8,128)(2,1)S(1)}, bf16[64,2048]{1,0:T(8,128)(2,1)S(1)}, u32[]{:S(2)}, u32[]{:S(2)}) collective-permute-start(bf16[64,2048]{1,0:T(8,128)(2,1)S(1)} %get-tuple-element.536), channel_id=1, source_target_pairs={{0,2},{1,3},{2,0},{3,1},{4,6},{5,7},{6,4},{7,5},{8,10},{9,11},{10,... | collective-permute-start | bytes 786440 | tf_op jit(solution)/shard_map/ppermute | solution.py:756
  97.8 7.3 %collective-permute-start.26 = (bf16[64,1024]{1,0:T(8,128)(2,1)S(1)}, bf16[64,1024]{1,0:T(8,128)(2,1)S(1)}, u32[]{:S(2)}, u32[]{:S(2)}) collective-permute-start(bf16[64,1024]{1,0:T(8,128)(2,1)S(1)} %shard_map.94.own_ref), channel_id=1, source_target_pairs={{0,1},{1,0},{2,3},{3,2},{4,5},{5,4},{6,7},{7,6},{8,9},{9,8},{10,11... | collective-permute-start | bytes 393224 | tf_op jit(solution)/shard_map/ppermute | solution.py:756
  99.1 8.5 %collective-permute-start.30 = (bf16[64,1024]{1,0:T(8,128)(2,1)S(1)}, bf16[64,1024]{1,0:T(8,128)(2,1)S(1)}, u32[]{:S(2)}, u32[]{:S(2)}) collective-permute-start(bf16[64,1024]{1,0:T(8,128)(2,1)S(1)} %shard_map.98.own_ref), channel_id=1, source_target_pairs={{0,1},{1,0},{2,3},{3,2},{4,5},{5,4},{6,7},{7,6},{8,9},{9,8},{10,11... | collective-permute-start | bytes 393224 | tf_op jit(solution)/shard_map/ppermute | solution.py:756
  102.1 10.2 %collective-permute-start.19 = (bf16[64,2048]{1,0:T(8,128)(2,1)S(1)}, bf16[64,2048]{1,0:T(8,128)(2,1)S(1)}, u32[]{:S(2)}, u32[]{:S(2)}) collective-permute-start(bf16[64,2048]{1,0:T(8,128)(2,1)S(1)} %get-tuple-element.548), channel_id=1, source_target_pairs={{0,2},{1,3},{2,0},{3,1},{4,6},{5,7},{6,4},{7,5},{8,10},{9,11},{10,... | collective-permute-start | bytes 786440 | tf_op jit(solution)/shard_map/ppermute | solution.py:756
  107.5 8.0 %collective-permute-start.27 = (bf16[64,2048]{1,0:T(8,128)(2,1)S(1)}, bf16[64,2048]{1,0:T(8,128)(2,1)S(1)}, u32[]{:S(2)}, u32[]{:S(2)}) collective-permute-start(bf16[64,2048]{1,0:T(8,128)(2,1)S(1)} %get-tuple-element.562), channel_id=1, source_target_pairs={{0,2},{1,3},{2,0},{3,1},{4,6},{5,7},{6,4},{7,5},{8,10},{9,11},{10,... | collective-permute-start | bytes 786440 | tf_op jit(solution)/shard_map/ppermute | solution.py:756
  107.6 10.7 %collective-permute-start.31 = (bf16[64,2048]{1,0:T(8,128)(2,1)S(1)}, bf16[64,2048]{1,0:T(8,128)(2,1)S(1)}, u32[]{:S(2)}, u32[]{:S(2)}) collective-permute-start(bf16[64,2048]{1,0:T(8,128)(2,1)S(1)} %shard_map.99), channel_id=1, source_target_pairs={{0,2},{1,3},{2,0},{3,1},{4,6},{5,7},{6,4},{7,5},{8,10},{9,11},{10,... | collective-permute-start | bytes 786440 | tf_op jit(solution)/shard_map/ppermute | solution.py:756
